TPU v7x, 32 devices: a 4x4x1 block of a 4x4x8 slice. The times are simulated.
32 devices in a mesh: dp: 1 (over z), sp: 32 (over y, x, core).
Axes of the slice: x: 4, y: 4, z: 1, core: 2. Of those that a mesh axis runs over, the one named last changes fastest.
The devices are a block of a 4x4x8 slice.
Arguments:
- x: bfloat16 [16, 2048], P('dp')
- lens: int32 [16], P('dp')
- wq: bfloat16 [2, 2048, 2048], replicated
- wk: bfloat16 [2, 2048, 256], replicated
- wv: bfloat16 [2, 2048, 256], replicated
- wo: bfloat16 [2, 2048, 2048], P(None, 'sp')
- w1: bfloat16 [2, 2048, 8192], P(None, None, 'sp')
- w2: bfloat16 [2, 8192, 2048], P(None, 'sp')
- g1: bfloat16 [2, 2048], replicated
- g2: bfloat16 [2, 2048], replicated
- kc: bfloat16 [2, 16, 16384, 4, 64], P(None, 'dp', 'sp')
- vc: bfloat16 [2, 16, 16384, 4, 64], P(None, 'dp', 'sp')
Outputs:
- output 1: bfloat16 [16, 2048], P('dp')
- output 2: bfloat16 [2, 16, 16384, 4, 64], P(None, 'dp', 'sp')
- output 3: bfloat16 [2, 16, 16384, 4, 64], P(None, 'dp', 'sp')
All inputs are finite; a program needn't handle non-finite values.
Results may differ from a plain program's by a relative error of at most 0.00880827.
Values are sent between devices in bfloat16 or wider.
A program may use at most 768 MiB of HBM per device.

v0:
```python
import jax
import jax.numpy as jnp
from jax import lax
from jax.sharding import PartitionSpec as P

EPS = 1e-6


def _rms(h, g):
    r = lax.rsqrt(jnp.mean(h * h, axis=-1, keepdims=True) + EPS)
    return (h * r * g.astype(jnp.float32)).astype(jnp.bfloat16)


def _mm(a, w):
    return jnp.dot(a, w, preferred_element_type=jnp.float32)


def solution(mesh):
    sp = mesh.shape['sp']
    kspec = P(None, 'dp', 'sp', None, None)

    def local(x, lens, wq, wk, wv, wo, w1, w2, g1, g2, kc, vc):
        nl, b, s_dev, kvh, dh = kc.shape
        hq = wq.shape[-1] // dh
        grp = hq // kvh
        hl = hq // sp
        idx = lax.axis_index('sp')
        posn = idx * s_dev + jnp.arange(s_dev)
        write = (posn[None, :] == (lens - 1)[:, None])[:, :, None, None]
        valid = (posn[None, :] < lens[:, None])[:, None, None, :]
        h = x.astype(jnp.float32)
        ks, vs = [], []
        for l in range(nl):
            xn = _rms(h, g1[l])
            q = _mm(xn, wq[l]).astype(jnp.bfloat16).reshape(b, kvh, grp, dh)
            k = _mm(xn, wk[l]).astype(jnp.bfloat16).reshape(b, 1, kvh, dh)
            v = _mm(xn, wv[l]).astype(jnp.bfloat16).reshape(b, 1, kvh, dh)
            kl = jnp.where(write, k, kc[l])
            vl = jnp.where(write, v, vc[l])
            ks.append(kl)
            vs.append(vl)
            s = jnp.einsum('bkgd,bskd->bkgs', q, kl, preferred_element_type=jnp.float32) * dh ** -0.5
            s = jnp.where(valid, s, -jnp.inf)
            m = jnp.max(s, axis=-1)
            p = jnp.exp(s - jnp.where(jnp.isfinite(m), m, 0.0)[..., None])
            den = jnp.sum(p, axis=-1)
            o = jnp.einsum('bkgs,bskd->bkgd', p.astype(jnp.bfloat16), vl, preferred_element_type=jnp.float32)
            c = jnp.exp(m - lax.pmax(m, 'sp'))
            o, den = lax.psum((o * c[..., None], den * c), 'sp')
            att = (o / den[..., None]).astype(jnp.bfloat16).reshape(b, hq, dh)
            att = lax.dynamic_slice_in_dim(att, idx * hl, hl, axis=1).reshape(b, hl * dh)
            h = h + lax.psum(_mm(att, wo[l]), 'sp')
            u = jax.nn.gelu(_mm(_rms(h, g2[l]), w1[l])).astype(jnp.bfloat16)
            h = h + lax.psum(_mm(u, w2[l]), 'sp')
        return h.astype(jnp.bfloat16), jnp.stack(ks), jnp.stack(vs)

    return jax.shard_map(
        local, mesh=mesh,
        in_specs=(P('dp', None), P('dp'), P(), P(), P(), P(None, 'sp', None), P(None, None, 'sp'),
                  P(None, 'sp', None), P(), P(), kspec, kspec),
        out_specs=(P('dp', None), kspec, kspec), check_vma=False)
```

profile of v0, /device:TPU:97, one launch (start us, length us, event | category | flops | bytes accessed | tf_op | source)
XLA Modules:
  0.0 708.6 jit_solution(7401027694610297204)
XLA Ops:
  9.7 1.6 convolution_convert_fusion.3
  11.3 4.7 fusion.18
  16.3 2.9 fusion.128
  19.3 49.9 %pmax.14 = f32[16,4,8]{2,1,0:T(4,128)S(1)} all-reduce(f32[16,4,8]{2,1,0:T(4,128)S(1)} %get-tuple-element.23), channel_id=1, replica_groups=mesh['dp'=1,'sp'=32] {'sp'}, use_global_device_ids=true, to_apply=%region_2.3 | all-reduce | flops 512 | bytes 4096 | tf_op jit(solution)/shard_map/pmax | solution.py:48
  70.0 4.3 fusion.32
  74.5 43.7 %psum.57 = f32[16,4,8]{2,1,0:T(4,128)S(1)} all-reduce(f32[16,4,8]{2,1,0:T(4,128)S(1)} %bitcast.113), channel_id=1, replica_groups=mesh['dp'=1,'sp'=32] {'sp'}, use_global_device_ids=true, to_apply=%region_5.6 | all-reduce | flops 512 | bytes 4096 | tf_op jit(solution)/shard_map/psum | solution.py:49
  118.2 47.3 %all-reduce.7.cloned.1.call-done = f32[16,4,8,64]{3,2,1,0:T(8,128)} async-done(((f32[16,4,8,64]{3,2,1,0:T(8,128)}), f32[16,4,8,64]{3,2,1,0:T(8,128)}) %all-reduce.7.cloned.1.call-update) | async-done | bytes 131088 | tf_op jit(solution)/shard_map/psum | solution.py:49
  166.6 1.8 fusion.64
  168.5 92.3 %all-reduce.9.cloned.1.call-done = f32[16,2048]{1,0:T(8,128)} async-done(((f32[16,2048]{1,0:T(8,128)}), f32[16,2048]{1,0:T(8,128)}) %all-reduce.9.cloned.1.call-update) | async-done | bytes 131088 | tf_op jit(solution)/shard_map/psum | solution.py:52
  261.9 2.8 fusion.40
  264.8 91.6 %all-reduce.11.cloned.1.call-done = f32[16,2048]{1,0:T(8,128)} async-done(((f32[16,2048]{1,0:T(8,128)}), f32[16,2048]{1,0:T(8,128)}) %all-reduce.11.cloned.1.call-update) | async-done | bytes 131088 | tf_op jit(solution)/shard_map/psum | solution.py:54
  360.5 4.6 fusion.21
  365.4 2.8 fusion.129
  368.2 45.8 %pmax.15 = f32[16,4,8]{2,1,0:T(4,128)S(1)} all-reduce(f32[16,4,8]{2,1,0:T(4,128)S(1)} %get-tuple-element.25), channel_id=1, replica_groups=mesh['dp'=1,'sp'=32] {'sp'}, use_global_device_ids=true, to_apply=%region_11.12 | all-reduce | flops 512 | bytes 4096 | tf_op jit(solution)/shard_map/pmax | solution.py:48
  414.5 4.2 fusion.33
  418.8 44.0 %psum.61 = f32[16,4,8]{2,1,0:T(4,128)S(1)} all-reduce(f32[16,4,8]{2,1,0:T(4,128)S(1)} %bitcast.114), channel_id=1, replica_groups=mesh['dp'=1,'sp'=32] {'sp'}, use_global_device_ids=true, to_apply=%region_14.15 | all-reduce | flops 512 | bytes 4096 | tf_op jit(solution)/shard_map/psum | solution.py:49
  462.8 46.7 %all-reduce.13.cloned.1.call-done = f32[16,4,8,64]{3,2,1,0:T(8,128)} async-done(((f32[16,4,8,64]{3,2,1,0:T(8,128)}), f32[16,4,8,64]{3,2,1,0:T(8,128)}) %all-reduce.13.cloned.1.call-update) | async-done | bytes 131088 | tf_op jit(solution)/shard_map/psum | solution.py:49
  510.6 1.8 fusion.62
  512.5 11.8 %broadcast_select_fusion.1 = (bf16[1,16,512,4,64]{2,4,3,1,0:T(8,128)(2,1)}, bf16[1,16,512,4,64]{2,4,3,1,0:T(8,128)(2,1)}, bf16[1,16,512,4,64]{2,4,3,1,0:T(8,128)(2,1)}, bf16[1,16,512,4,64]{2,4,3,1,0:T(8,128)(2,1)}) fusion(pred[16,512]{1,0:T(8,128)(4,1)S(1)} %get-tuple-element.22, bf16[2,16,512,4,64]{2,4,3,1,0:T(8,128)(2,1)} %param.23, ...), kind=kLoop, calls=%fused_computation.17 | loop fusion | flops 8388608 | bytes 33595392 | tf_op jit(solution)/shard_map/jit(_where)/select_n | solution.py:39
  524.3 80.4 %all-reduce.15.cloned.1.call-done = f32[16,2048]{1,0:T(8,128)} async-done(((f32[16,2048]{1,0:T(8,128)}), f32[16,2048]{1,0:T(8,128)}) %all-reduce.15.cloned.1.call-update) | async-done | bytes 131088 | tf_op jit(solution)/shard_map/psum | solution.py:52
  605.8 2.7 fusion.34
  608.5 11.6 %pad_maximum_fusion = (bf16[2,16,512,4,64]{2,4,3,1,0:T(8,128)(2,1)}, bf16[2,16,512,4,64]{2,4,3,1,0:T(8,128)(2,1)}) fusion(bf16[1,16,512,4,64]{2,4,3,1,0:T(8,128)(2,1)} %get-tuple-element.15, bf16[1,16,512,4,64]{2,4,3,1,0:T(8,128)(2,1)} %get-tuple-element.16, bf16[1,16,512,4,64]{2,4,3,1,0:T(8,128)(2,1)} %get-tuple-element.12, ...), kind=kLoop, calls=%fused_computation | loop fusion | flops 8388608 | bytes 33554432 | tf_op jit(solution)/shard_map/stack | solution.py:55
  620.0 80.1 %all-reduce.17.cloned.1.call-done = f32[16,2048]{1,0:T(8,128)} async-done(((f32[16,2048]{1,0:T(8,128)}), f32[16,2048]{1,0:T(8,128)}) %all-reduce.17.cloned.1.call-update) | async-done | bytes 131088 | tf_op jit(solution)/shard_map/psum | solution.py:54
  700.2 1.5 add_convert_fusion
  (55 shorter events, 13.5 us)
Async XLA Ops:
  7.2 158.3 %all-reduce.7.cloned.1.call-start = ((), (), s32[]{:S(2)}) async-start(), calls=%async_computation | async-start | bytes 524288 | tf_op jit(solution)/shard_map/psum | solution.py:49
  11.3 4.9 copy-start.4
  16.3 52.9 %copy-start.1 = (bf16[16,2048]{1,0:T(8,128)(2,1)S(1)}, bf16[16,2048]{1,0:T(8,128)(2,1)}, u32[]{:S(2)}) copy-start(bf16[16,2048]{1,0:T(8,128)(2,1)} %param.12) | copy-start | bytes 196612
  16.3 52.9 %copy-start.2 = (bf16[2,2048,256]{2,1,0:T(8,128)(2,1)S(1)}, bf16[2,2048,256]{2,1,0:T(8,128)(2,1)}, u32[]{:S(2)}) copy-start(bf16[2,2048,256]{2,1,0:T(8,128)(2,1)} %param.16) | copy-start | bytes 6291460
  70.0 98.5 %copy-start.3 = (bf16[2,2048]{1,0:T(2,128)(2,1)S(1)}, bf16[2,2048]{1,0:T(2,128)(2,1)}, u32[]{:S(2)}) copy-start(bf16[2,2048]{1,0:T(2,128)(2,1)} %param.21) | copy-start | bytes 24580
  70.0 191.9 %copy-start = (bf16[2,256,2048]{2,1,0:T(8,128)(2,1)S(1)}, bf16[2,256,2048]{2,1,0:T(8,128)(2,1)}, u32[]{:S(2)}) copy-start(bf16[2,256,2048]{2,1,0:T(8,128)(2,1)} %param.19) | copy-start | bytes 6291460
  74.4 186.5 %all-reduce.9.cloned.1.call-start = ((), (), s32[]{:S(2)}) async-start(), calls=%async_computation.1 | async-start | bytes 262144 | tf_op jit(solution)/shard_map/psum | solution.py:52
  168.4 188.0 %all-reduce.11.cloned.1.call-start = ((), (), s32[]{:S(2)}) async-start(), calls=%async_computation.2 | async-start | bytes 262144 | tf_op jit(solution)/shard_map/psum | solution.py:54
  264.7 244.8 %all-reduce.13.cloned.1.call-start = ((), (), s32[]{:S(2)}) async-start(), calls=%async_computation.3 | async-start | bytes 524288 | tf_op jit(solution)/shard_map/psum | solution.py:49
  418.7 186.0 %all-reduce.15.cloned.1.call-start = ((), (), s32[]{:S(2)}) async-start(), calls=%async_computation.4 | async-start | bytes 262144 | tf_op jit(solution)/shard_map/psum | solution.py:52
  512.4 187.7 %all-reduce.17.cloned.1.call-start = ((), (), s32[]{:S(2)}) async-start(), calls=%async_computation.5 | async-start | bytes 262144 | tf_op jit(solution)/shard_map/psum | solution.py:54
Sparse Core Ops, SparseCore 0:
  74.5 90.9 all-reduce.6
  169.3 91.4 all-reduce.8
  264.8 91.5 all-reduce.10
  418.8 90.6 all-reduce.12
  513.2 91.4 all-reduce.14
  608.6 91.5 all-reduce.16
where the time goes:
time: 710 us; the launch traced here: 709 us
  waiting for transfers between devices  439 us (62%)
  blocking collectives  183 us (26%)
  matrix products  37.2 us (5%)
  other arithmetic  33.6 us (5%)
  between operations  14.3 us (2%)
    psum x2, waiting for transfers between devices, local(): h = h + lax.psum(_mm(att, wo[l]), 'sp')  173 us
    psum x2, waiting for transfers between devices, local(): h = h + lax.psum(_mm(u, w2[l]), 'sp')  172 us
    pmax x2, blocking collectives, local(): c = jnp.exp(m - lax.pmax(m, 'sp'))  95.7 us
    psum x2, waiting for transfers between devices, local(): o, den = lax.psum((o * c[..., None], den * c), 'sp')  94 us
    psum x2, blocking collectives, local(): o, den = lax.psum((o * c[..., None], den * c), 'sp')  87.7 us
    dot_general x10, matrix products, _mm(): return jnp.dot(a, w, preferred_element_type=jnp.float32)  23 us
  transfers between devices with their start and end apart: 6, of which 6 were waited for; matrix products, arithmetic and copies ran while one was open for 3% of the time, Pallas kernels for 0%

commit v1 on v0

v1 whole, which is shorter than its diff:
```python
import functools

import jax
import jax.numpy as jnp
from jax import lax
from jax.experimental import pallas as pl
from jax.experimental.pallas import tpu as pltpu
from jax.sharding import PartitionSpec as P

EPS = 1e-6
LANES = 128
SUB = 8
NEG = float(jnp.finfo(jnp.float32).min)
F32 = jnp.float32
BF16 = jnp.bfloat16
MESH = pl.DeviceIdType.MESH
QCH = 4


def _dot(a, w):
    return jnp.dot(a, w, preferred_element_type=F32)


def _step_kernel(n, dims, lens_ref, x_ref, g1_ref, g2_ref, wq, wk, wv, wo, w1, w2, kc, vc,
                 y_ref, kn_out, vn_out,
                 wq_v, wk_v, wv_v, wo_v, w1_v, w2_v, k_v, v_v, qs, kn, vn, xn, hb, hown,
                 asend, arecv, s1, r1, s2, r2, lsem, ssem, rsem):
    nl, nb, s_dev, kvd, dh = dims
    D = x_ref.shape[1]
    nc = n // 2
    me = lax.axis_index('sp')
    par = lax.rem(me, 2)
    half = nb // 2

    cw = D // QCH

    def loads(l):
        out = {}
        i = 0

        def add(name, src, dst):
            nonlocal i
            out[name] = pltpu.make_async_copy(src, dst, lsem.at[l, i])
            i += 1
        add('wk', wk.at[l], wk_v.at[l])
        add('wv', wv.at[l], wv_v.at[l])
        for j in range(QCH):
            add(f'wq{j}', wq.at[l, :, pl.ds(j * cw, cw)], wq_v.at[l, :, pl.ds(j * cw, cw)])
        for j in range(2):
            add(f'k{j}', kc.at[l, pl.ds(j * half, half)], k_v.at[l, pl.ds(j * half, half)])
            add(f'v{j}', vc.at[l, pl.ds(j * half, half)], v_v.at[l, pl.ds(j * half, half)])
        add('wo', wo.at[l], wo_v.at[l, pl.ds(pl.multiple_of(par * dh, dh), dh)])
        add('w1', w1.at[l], w1_v.at[l])
        add('w2', w2.at[l], w2_v.at[l])
        return out

    ld = [loads(l) for l in range(nl)]
    for c in ld[0].values():
        c.start()

    bar = pltpu.get_barrier_semaphore()

    def sig(k, carry):
        pl.semaphore_signal(bar, 1, device_id={'sp': lax.rem(me + k, n)}, device_id_type=MESH)
        return carry
    lax.fori_loop(1, n, sig, 0)

    def send_all(src_of, dst, phase, step=1):
        def body(k, carry):
            d = lax.rem(me + k * step, n)
            pltpu.make_async_remote_copy(src_of(d), dst, ssem.at[phase], rsem.at[phase],
                                         device_id={'sp': d}, device_id_type=MESH).start()
            return carry
        lax.fori_loop(1, n // step, body, 0)

    def wait_recv(buf, count, phase):
        r = buf.at[pl.ds(0, count)]
        pltpu.make_async_copy(r, r, rsem.at[phase]).wait()

    def wait_send(buf, count, phase):
        r = buf.at[pl.ds(0, count)]
        pltpu.make_async_copy(r, r, ssem.at[phase]).wait()

    lane = lax.broadcasted_iota(jnp.int32, (SUB, LANES), 1)
    row = lax.broadcasted_iota(jnp.int32, (SUB, LANES), 0)
    lo = lane < dh
    quart = lax.rem(lane, dh) < dh // 2
    ma = (row < SUB // 2) & lo
    mb = (row >= SUB // 2) & (~lo)
    col = lax.broadcasted_iota(jnp.int32, (2 * nc, s_dev), 1)
    off = me * s_dev

    def rms_to_xn(st, g_ref, l):
        for r in range(2):
            ss = None
            for c in range(nc):
                t = hb[st, 2 * c + r]
                ss = t * t if ss is None else ss + t * t
            rr = lax.rsqrt(jnp.sum(ss, axis=1, keepdims=True) / D + EPS)
            for c in range(nc):
                g = g_ref[l:l + 1, c * LANES:(c + 1) * LANES].astype(F32)
                xn[r * SUB:(r + 1) * SUB, c * LANES:(c + 1) * LANES] = (hb[st, 2 * c + r] * rr * g).astype(BF16)

    for c in range(nc):
        for r in range(2):
            hb[0, 2 * c + r] = x_ref[r * SUB:(r + 1) * SUB, c * LANES:(c + 1) * LANES].astype(F32)
    h = hb[0, me]

    ph = 0
    st = 0
    for l in range(nl):
        rms_to_xn(st, g1_ref, l)
        ld[l]['wk'].wait()
        ld[l]['wv'].wait()
        kn[...] = _dot(xn[...], wk_v[l]).astype(BF16).astype(F32)
        vn[...] = _dot(xn[...], wv_v[l]).astype(BF16).astype(F32)
        for j in range(QCH):
            ld[l][f'wq{j}'].wait()
            q = _dot(xn[...], wq_v[l, :, j * cw:(j + 1) * cw]).astype(BF16).astype(F32)
            for t in range(cw // LANES):
                c = j * (cw // LANES) + t
                for r in range(2):
                    qs[pl.ds(r * SUB * nc + c, SUB, stride=nc), :] = q[r * SUB:(r + 1) * SUB, t * LANES:(t + 1) * LANES]

        for r in range(2):
            ld[l][f'k{r}'].wait()
            ld[l][f'v{r}'].wait()
            for bb in range(half):
                b = r * half + bb
                xq = qs[b * nc:(b + 1) * nc, :]
                xr = pltpu.roll(xq, dh, 1)
                z = jnp.zeros((SUB, LANES), F32)
                parts = []
                for a, o in ((xq, xr), (xr, xq)):
                    e0 = jnp.where(ma, a[0:SUB], jnp.where(mb, o[0:SUB], 0.0))
                    e1 = jnp.where(ma, a[SUB:], jnp.where(mb, o[SUB:], 0.0))
                    parts.append(jnp.concatenate([e0, z], axis=1))
                    parts.append(jnp.concatenate([z, e1], axis=1))
                qf = jnp.concatenate(parts, axis=0)
                pb = lens_ref[b] - 1 - off
                s = _dot(qf.astype(BF16), k_v[l, b]) * dh ** -0.5
                sn = jnp.sum(qf * kn[b:b + 1, :], axis=1, keepdims=True) * dh ** -0.5
                s = jnp.where(col < pb, s, jnp.where(col == pb, sn, -jnp.inf))
                m = jnp.maximum(jnp.max(s, axis=1, keepdims=True), NEG)
                p = jnp.exp(s - m)
                den = jnp.sum(p, axis=1, keepdims=True)
                inside = jnp.logical_and(pb >= 0, pb < s_dev)
                pn = jnp.where(inside, jnp.exp(sn - m), 0.0)
                pz = jnp.where(col == pb, 0.0, p).astype(BF16)
                o = lax.dot_general(pz, v_v[l, b], (((1,), (1,)), ((), ())), preferred_element_type=F32)
                o = o + pn * vn[b:b + 1, :]
                for t in range(2):
                    ev = o[t * SUB:(t + 1) * SUB, t * LANES:(t + 1) * LANES]
                    od = o[nc + t * SUB:nc + (t + 1) * SUB, t * LANES:(t + 1) * LANES]
                    evr = pltpu.roll(ev, dh, 1)
                    odr = pltpu.roll(od, dh, 1)
                    tile = jnp.where(row < SUB // 2, jnp.where(lo, ev, odr), jnp.where(lo, evr, od))
                    me_, le_ = m[t * SUB:(t + 1) * SUB], den[t * SUB:(t + 1) * SUB]
                    mo_, lo_ = m[nc + t * SUB:nc + (t + 1) * SUB], den[nc + t * SUB:nc + (t + 1) * SUB]
                    stat = jnp.where(lo, jnp.where(quart, me_, le_), jnp.where(quart, mo_, lo_))
                    base = (2 * SUB * t + r) * 2 * SUB + bb
                    asend[l, pl.ds(base, SUB, stride=4 * SUB), :] = tile
                    asend[l, pl.ds(base + SUB, SUB, stride=4 * SUB), :] = stat
        if l == 0:
            pl.semaphore_wait(bar, n - 1)
        send_all(lambda d: asend.at[l, pl.ds(pl.multiple_of(d * 2 * SUB, 2 * SUB), 2 * SUB)], arecv.at[l, me], ph)
        if l == 0:
            other = me + 1 - 2 * par
            wo_x = []
            for ll in range(nl):
                cp = pltpu.make_async_remote_copy(
                    wo.at[ll], wo_v.at[ll, pl.ds(pl.multiple_of(par * dh, dh), dh)],
                    ssem.at[5 * nl + ll], rsem.at[5 * nl + ll], device_id={'sp': other}, device_id_type=MESH)
                cp.start()
                wo_x.append(cp)
            for cp in ld[1].values():
                cp.start()
        arecv[l, me] = asend[l, pl.ds(pl.multiple_of(me * 2 * SUB, 2 * SUB), 2 * SUB), :]
        pad = jnp.zeros((LANES - nb, kvd), F32)
        kn_out[l] = jnp.concatenate([kn[...], pad], axis=0).T
        vn_out[l] = jnp.concatenate([vn[...], pad], axis=0).T
        wait_recv(arecv.at[l], n - 1, ph)
        ph += 1

        mx = None
        for i in range(n):
            sa = arecv[l, i, SUB:]
            mt = jnp.where(quart, sa, pltpu.roll(sa, dh // 2, 1))
            mx = mt if mx is None else jnp.maximum(mx, mt)
        num = jnp.zeros((SUB, LANES), F32)
        den = jnp.zeros((SUB, LANES), F32)
        for i in range(n):
            sa = arecv[l, i, SUB:]
            mt = jnp.where(quart, sa, pltpu.roll(sa, dh // 2, 1))
            dt = jnp.where(quart, pltpu.roll(sa, LANES - dh // 2, 1), sa)
            w = jnp.exp(mt - mx)
            den = den + w * dt
            num = num + w * arecv[l, i, 0:SUB]
        att = (num / den).astype(BF16)

        ld[l]['wo'].wait()
        wo_x[l].wait()
        part = _dot(att, wo_v[l])
        for c in range(nc):
            s1[l, c] = part[:, c * LANES:(c + 1) * LANES]
        mc = lax.div(me, 2)
        send_all(lambda d: s1.at[l, lax.div(d, 2)], r1.at[l, mc], ph, 2)
        r1[l, mc] = s1[l, mc]
        wait_recv(r1.at[l], nc - 1, ph)
        ph += 1
        tot = r1[l, 0]
        for c in range(1, nc):
            tot = tot + r1[l, c]
        h = h + tot

        def gather(h):
            hown[st] = h
            send_all(lambda d: hown.at[st], hb.at[st + 1, me], ph)
            hb[st + 1, me] = h
            wait_recv(hb.at[st + 1], n - 1, ph)
        gather(h)
        ph += 1
        st += 1

        rms_to_xn(st, g2_ref, l)
        ld[l]['w1'].wait()
        u = jax.nn.gelu(_dot(xn[...], w1_v[l]), approximate=True).astype(BF16)
        ld[l]['w2'].wait()
        part = _dot(u, w2_v[l])
        for c in range(nc):
            for r in range(2):
                s2[l, 2 * c + r] = part[r * SUB:(r + 1) * SUB, c * LANES:(c + 1) * LANES]
        send_all(lambda d: s2.at[l, d], r2.at[l, me], ph)
        r2[l, me] = s2[l, me]
        wait_recv(r2.at[l], n - 1, ph)
        ph += 1
        tot = r2[l, 0]
        for d in range(1, n):
            tot = tot + r2[l, d]
        h = h + tot
        gather(h)
        ph += 1
        st += 1

    for c in range(nc):
        for r in range(2):
            y_ref[r * SUB:(r + 1) * SUB, c * LANES:(c + 1) * LANES] = hb[st, 2 * c + r].astype(BF16)

    for l in range(nl):
        wait_send(arecv.at[l], n - 1, 5 * l)
        wait_send(r1.at[l], nc - 1, 5 * l + 1)
        wait_send(hb.at[0], n - 1, 5 * l + 2)
        wait_send(r2.at[l], n - 1, 5 * l + 3)
        wait_send(hb.at[0], n - 1, 5 * l + 4)


def _cache_kernel(s_dev, per, lens_ref, y_ref, kn_ref, vn_ref, k_ref, v_ref, y_out, k_out, v_out):
    off = lax.axis_index('sp') * s_dev
    g = pl.program_id(1)
    y_out[...] = y_ref[...]
    lane = lax.broadcasted_iota(jnp.int32, kn_ref.shape[1:], 1)
    col = lax.broadcasted_iota(jnp.int32, k_ref.shape[2:], 1)
    for i in range(per):
        b = g * per + i
        pb = lens_ref[b] - 1 - off
        for new, src, dst in ((kn_ref, k_ref, k_out), (vn_ref, v_ref, v_out)):
            c = jnp.sum(jnp.where(lane == b, new[0], 0.0), axis=1, keepdims=True)
            dst[0, i] = jnp.where(col == pb, c, src[0, i].astype(F32)).astype(BF16)


def solution(mesh):
    n = mesh.shape['sp']
    kspec = P(None, 'dp', 'sp', None, None)

    def local(x, lens, wq, wk, wv, wo, w1, w2, g1, g2, kc, vc):
        nl, nb, s_dev, kvh, dh = kc.shape
        D = x.shape[1]
        kvd = kvh * dh
        ff = w1.shape[2]
        nc = n // 2
        kt = jnp.transpose(kc, (0, 1, 3, 4, 2)).reshape(nl, nb, kvd, s_dev)
        vt = jnp.transpose(vc, (0, 1, 3, 4, 2)).reshape(nl, nb, kvd, s_dev)
        vm = pl.BlockSpec(memory_space=pltpu.VMEM)
        anys = pl.BlockSpec(memory_space=pl.ANY)
        y, kn, vn = pl.pallas_call(
            functools.partial(_step_kernel, n, (nl, nb, s_dev, kvd, dh)),
            out_shape=(jax.ShapeDtypeStruct((nb, D), BF16),
                       jax.ShapeDtypeStruct((nl, kvd, LANES), F32),
                       jax.ShapeDtypeStruct((nl, kvd, LANES), F32)),
            in_specs=[pl.BlockSpec(memory_space=pltpu.SMEM), vm, vm, vm] + [anys] * 8,
            out_specs=(vm, vm, vm),
            scratch_shapes=[
                pltpu.VMEM((nl, D, D), BF16),
                pltpu.VMEM((nl, D, kvd), BF16),
                pltpu.VMEM((nl, D, kvd), BF16),
                pltpu.VMEM((nl, 2 * dh, D), BF16),
                pltpu.VMEM((nl, D, ff), BF16),
                pltpu.VMEM((nl, ff, D), BF16),
                pltpu.VMEM((nl, nb, kvd, s_dev), BF16),
                pltpu.VMEM((nl, nb, kvd, s_dev), BF16),
                pltpu.VMEM((nb * nc, LANES), F32),
                pltpu.VMEM((nb, kvd), F32),
                pltpu.VMEM((nb, kvd), F32),
                pltpu.VMEM((nb, D), BF16),
                pltpu.VMEM((2 * nl + 1, n, SUB, LANES), F32),
                pltpu.VMEM((2 * nl, SUB, LANES), F32),
                pltpu.VMEM((nl, n * 2 * SUB, LANES), F32),
                pltpu.VMEM((nl, n, 2 * SUB, LANES), F32),
                pltpu.VMEM((nl, nc, SUB, LANES), F32),
                pltpu.VMEM((nl, nc, SUB, LANES), F32),
                pltpu.VMEM((nl, n, SUB, LANES), F32),
                pltpu.VMEM((nl, n, SUB, LANES), F32),
                pltpu.SemaphoreType.DMA((nl, QCH + 9)),
                pltpu.SemaphoreType.DMA((6 * nl,)),
                pltpu.SemaphoreType.DMA((6 * nl,)),
            ],
            compiler_params=pltpu.CompilerParams(
                collective_id=0, has_side_effects=True, vmem_limit_bytes=60 * 1024 * 1024),
        )(lens, x, g1, g2, wq, wk, wv, wo, w1, w2, kt, vt)

        per = 2
        cspec = pl.BlockSpec((1, per, kvd, s_dev), lambda l, g: (l, g, 0, 0))
        nspec = pl.BlockSpec((1, kvd, LANES), lambda l, g: (l, 0, 0))
        yspec = pl.BlockSpec((nb, D), lambda l, g: (0, 0))
        y, k2, v2 = pl.pallas_call(
            functools.partial(_cache_kernel, s_dev, per),
            out_shape=(jax.ShapeDtypeStruct((nb, D), BF16), jax.ShapeDtypeStruct(kt.shape, BF16),
                       jax.ShapeDtypeStruct(vt.shape, BF16)),
            grid=(nl, nb // per),
            in_specs=[pl.BlockSpec(memory_space=pltpu.SMEM), yspec, nspec, nspec, cspec, cspec],
            out_specs=(yspec, cspec, cspec),
        )(lens, y, kn, vn, kt, vt)

        def back(a):
            return jnp.transpose(a.reshape(nl, nb, kvh, dh, s_dev), (0, 1, 4, 2, 3))
        return y, back(k2), back(v2)

    return jax.shard_map(
        local, mesh=mesh,
        in_specs=(P('dp', None), P('dp'), P(), P(), P(), P(None, 'sp', None), P(None, None, 'sp'),
                  P(None, 'sp', None), P(), P(), kspec, kspec),
        out_specs=(P('dp', None), kspec, kspec), check_vma=False)
```

time: 710 us -> 96 us (0.14)
  waiting for transfers between devices: 439 us -> 0 us
  blocking collectives: 183 us -> 0 us
  Pallas kernels: 0 us -> 94.8 us
  matrix products: 37.2 us -> 0 us
  other arithmetic: 33.6 us -> 0 us
  between operations: 14.3 us -> 0.64 us
    psum x6 -> x0, waiting for transfers between devices: 438 us -> none  [the longest x2 173 us: local(): h = h + lax.psum(_mm(att, wo[l]), 'sp')]
    pmax x2 -> x0, blocking collectives: 95.7 us -> none  [local(): c = jnp.exp(m - lax.pmax(m, 'sp'))]
    pallas_call x0 -> x2, Pallas kernels: none -> 94.8 us  [the longest x1 76.2 us: local(): pl.pallas_call(functools.partial(_step_kernel, n, (nl, nb, s_dev, kvd, dh...]
    psum x2 -> x0, blocking collectives: 87.7 us -> none  [local(): o, den = lax.psum((o * c[..., None], den * c), 'sp')]
    dot_general x14 -> x0, matrix products: 37.2 us -> none  [the longest x10 23 us: _mm(): return jnp.dot(a, w, preferred_element_type=jnp.float32)]
    select_n x3 -> x0, other arithmetic: 11.8 us -> none  [the longest x1 11.8 us: local(): vl = jnp.where(write, v, vc[l])]
    another operation x1 -> x0, other arithmetic: 11.6 us -> none  [local(): return (h.astype(jnp.bfloat16), jnp.stack(ks), jnp.stack(vs))]
  transfers between devices with their start and end apart: 6 -> 0, of which waited for: 6 -> 0; matrix products, arithmetic and copies ran while one was open for 3% -> 0% of each run, Pallas kernels for 0% -> 0%
where the time goes in v1:
time: 96 us; the launch traced here: 95.4 us
  Pallas kernels  94.8 us (99%)
    pallas_call x1, Pallas kernels, local(): pl.pallas_call(functools.partial(_step_kernel, n, (nl, nb, s_dev, kvd, dh...  76.2 us
    pallas_call x1, Pallas kernels, local(): pl.pallas_call(functools.partial(_cache_kernel, s_dev, per), out_shape=(j...  18.6 us

profile of v1, /device:TPU:97, one launch (start us, length us, event | category | flops | bytes accessed | tf_op | source)
XLA Modules:
  0.0 95.4 jit_solution(4930617082644963410)
XLA Ops:
  0.6 76.2 %shard_map.139 = (bf16[16,2048]{1,0:T(8,128)(2,1)}, f32[2,256,128]{2,1,0:T(8,128)}, f32[2,256,128]{2,1,0:T(8,128)}) custom-call(s32[16]{0:T(128)} %lens_ref.3, bf16[16,2048]{1,0:T(8,128)(2,1)} %x_ref.1, bf16[2,2048]{1,0:T(2,128)(2,1)} %g1_ref.1, bf16[2,2048]{1,0:T(2,128)(2,1)} %g2_ref.1, bf16[2,2048,2048]{2,1,0:T(8,128)(2,1)} %wq.1, ...), custom_call_target="tpu_custom_call" | custom-call | tf_op jit(solution)/shard_map/pallas_call | solution.py:285
  76.8 18.6 %shard_map.140 = (bf16[16,2048]{1,0:T(8,128)(2,1)}, bf16[2,16,256,512]{3,2,1,0:T(8,128)(2,1)}, bf16[2,16,256,512]{3,2,1,0:T(8,128)(2,1)}) custom-call(s32[16]{0:T(128)} %lens_ref.3, bf16[16,2048]{1,0:T(8,128)(2,1)} %get-tuple-element.9.y_ref, f32[2,256,128]{2,1,0:T(8,128)} %get-tuple-element.10.kn_ref, f32[2,256,128]{2,1,0:T(8,128)} %get-tuple-element.11.vn_ref, ...), custom_call_target="tpu_custom_call" | custom-call | tf_op jit(solution)/shard_map/pallas_call | solution.py:325

commit v2 on v0

v2 whole, which is shorter than its diff:
```python
import functools

import jax
import jax.numpy as jnp
from jax import lax
from jax.experimental import pallas as pl
from jax.experimental.pallas import tpu as pltpu
from jax.sharding import PartitionSpec as P

EPS = 1e-6
LANES = 128
SUB = 8
NEG = float(jnp.finfo(jnp.float32).min)
F32 = jnp.float32
BF16 = jnp.bfloat16
MESH = pl.DeviceIdType.MESH
QCH = 4
OWN = 1
STW = 32


def _dot(a, w):
    return jnp.dot(a, w, preferred_element_type=F32)


def _step_kernel(n, dims, lens, x, g1, g2, wq, wk, wv, wo, w1, w2, kc, vc,
                 y_ref, k_v, v_v,
                 wq_v, wk_v, wv_v, wo_v, w1_v, w2_v, x_v, g1_v, g2_v, lens_v, qs, kn, vn, knt, vnt, xn, hb, hs,
                 os, orv, ss, sr, s1, r1, s2, r2, lsem, ssem, rsem):
    nl, nb, s_dev, kvd, dh = dims
    D = x_v.shape[1]
    nc = n // 2
    me = lax.axis_index('sp')
    par = lax.rem(me, 2)
    mc = lax.div(me, 2)
    own = par == OWN
    other = me + 1 - 2 * par

    cw = D // QCH

    def loads(l):
        out = {}
        i = 0

        def add(name, src, dst):
            nonlocal i
            out[name] = pltpu.make_async_copy(src, dst, lsem.at[l, i])
            i += 1
        if l == 0:
            add('x', x, x_v)
            add('g1', g1, g1_v)
            add('lens', lens, lens_v)
        add('wk', wk.at[l], wk_v.at[l])
        add('wv', wv.at[l], wv_v.at[l])
        for j in range(QCH):
            add(f'wq{j}', wq.at[l, :, pl.ds(j * cw, cw)], wq_v.at[l, :, pl.ds(j * cw, cw)])
        for j in range(2):
            add(f'k{j}', kc.at[l, pl.ds(j * SUB, SUB)], k_v.at[l, pl.ds(j * SUB, SUB)])
            add(f'v{j}', vc.at[l, pl.ds(j * SUB, SUB)], v_v.at[l, pl.ds(j * SUB, SUB)])
        if l == 0:
            add('g2', g2, g2_v)
        add('w1', w1.at[l], w1_v.at[l])
        add('w2', w2.at[l], w2_v.at[l])
        return out

    ld = [loads(l) for l in range(nl)]
    for c in ld[0].values():
        c.start()

    bar = pltpu.get_barrier_semaphore()

    def sig(k, carry):
        pl.semaphore_signal(bar, 1, device_id={'sp': lax.rem(me + k, n)}, device_id_type=MESH)
        return carry
    lax.fori_loop(1, n, sig, 0)

    A2A, STAT, RS1, AG1, RS2, AG2, WO = range(7)

    def sem(l, r, kind):
        return (l * 2 + r) * 7 + kind

    def rcopy(src, dst, i, d):
        return pltpu.make_async_remote_copy(src, dst, ssem.at[i], rsem.at[i], device_id={'sp': d}, device_id_type=MESH)

    def to_owners(pairs):
        def body(k, carry):
            c = lax.rem(mc + k, nc)
            for src, dst, i in pairs:
                rcopy(src(c), dst, i, 2 * c + OWN).start()
            return carry
        lax.fori_loop(1, nc, body, 0)

        @pl.when(jnp.logical_not(own))
        def _():
            body(0, 0)

    def wait(ref, count, s):
        r = ref.at[pl.ds(0, count)]
        pltpu.make_async_copy(r, r, s).wait()

    lane = lax.broadcasted_iota(jnp.int32, (SUB, LANES), 1)
    row = lax.broadcasted_iota(jnp.int32, (SUB, LANES), 0)
    lo = lane < dh
    ma = (row < SUB // 2) & lo
    mb = (row >= SUB // 2) & (~lo)
    col = lax.broadcasted_iota(jnp.int32, (2 * nc, s_dev), 1)
    col1 = lax.broadcasted_iota(jnp.int32, (1, s_dev), 1)
    off = me * s_dev

    def normed(st, r, g_v, l):
        ss_ = None
        for c in range(nc):
            t = hb[st, r, c]
            ss_ = t * t if ss_ is None else ss_ + t * t
        rr = lax.rsqrt(jnp.sum(ss_, axis=1, keepdims=True) / D + EPS)
        for c in range(nc):
            g = g_v[l:l + 1, c * LANES:(c + 1) * LANES].astype(F32)
            xn[r, :, c * LANES:(c + 1) * LANES] = (hb[st, r, c] * rr * g).astype(BF16)

    def gather(l, st, r, kind, h):
        hs[st, r] = h

        def body(k, carry):
            rcopy(hs.at[st, r], hb.at[st + 1, r, mc], sem(l, r, kind), lax.rem(me + k, n)).start()
            return carry
        lax.fori_loop(1, n, body, 0)
        hb[st + 1, r, mc] = h

    def gathered(l, st, r, kind):
        @pl.when(own)
        def _():
            wait(hb.at[st + 1, r], nc - 1, rsem.at[sem(l, r, kind)])

        @pl.when(jnp.logical_not(own))
        def _():
            wait(hb.at[st + 1, r], nc, rsem.at[sem(l, r, kind)])

    def put_new(l, new_t, ref):
        for b in range(nb):
            pb = lens_v[b] - 1 - off
            hit = jnp.where(col1 == pb, 1.0, 0.0).astype(BF16)
            c = jnp.broadcast_to(new_t[:, b:b + 1], (kvd, LANES)).astype(BF16)
            for t in range(s_dev // LANES):
                sl = slice(t * LANES, (t + 1) * LANES)
                hm = jnp.broadcast_to(hit[:, sl], (kvd, LANES)) > 0.5
                ref[l, b, :, sl] = jnp.where(hm, c, ref[l, b, :, sl])

    ld[0]['x'].wait()
    for c in range(nc):
        for r in range(2):
            hb[0, r, c] = x_v[r * SUB:(r + 1) * SUB, c * LANES:(c + 1) * LANES].astype(F32)
    ld[0]['g1'].wait()

    wo_in = [rcopy(wo.at[ll], wo_v.at[ll, pl.ds((1 - OWN) * dh, dh)], sem(ll, 0, WO), other) for ll in range(nl)]
    wo_my = [pltpu.make_async_copy(wo.at[ll], wo_v.at[ll, pl.ds(OWN * dh, dh)], lsem.at[ll, QCH + 12])
             for ll in range(nl)]
    st = 0
    for l in range(nl):
        for r in range(2):
            if l > 0:
                gathered(l - 1, st - 1, r, AG2)
            normed(st, r, g1_v, l)
            if r == 0:
                ld[l]['wk'].wait()
                ld[l]['wv'].wait()
            kn[r] = _dot(xn[r], wk_v[l]).astype(BF16).astype(F32)
            vn[r] = _dot(xn[r], wv_v[l]).astype(BF16).astype(F32)
            for j in range(QCH):
                if r == 0:
                    ld[l][f'wq{j}'].wait()
                q = _dot(xn[r], wq_v[l, :, j * cw:(j + 1) * cw]).astype(BF16).astype(F32)
                for t in range(cw // LANES):
                    qs[r, pl.ds(j * (cw // LANES) + t, SUB, stride=nc), :] = q[:, t * LANES:(t + 1) * LANES]

            if l == 0 and r == 0:
                ld[0]['lens'].wait()
            ld[l][f'k{r}'].wait()
            ld[l][f'v{r}'].wait()
            stats = [jnp.zeros((SUB, LANES), F32) for _ in range(2)]
            for bb in range(SUB):
                b = r * SUB + bb
                xq = qs[r, bb * nc:(bb + 1) * nc, :]
                xr = pltpu.roll(xq, dh, 1)
                z = jnp.zeros((SUB, LANES), F32)
                parts = []
                for a, o in ((xq, xr), (xr, xq)):
                    e0 = jnp.where(ma, a[0:SUB], jnp.where(mb, o[0:SUB], 0.0))
                    e1 = jnp.where(ma, a[SUB:], jnp.where(mb, o[SUB:], 0.0))
                    parts.append(jnp.concatenate([e0, z], axis=1))
                    parts.append(jnp.concatenate([z, e1], axis=1))
                qf = jnp.concatenate(parts, axis=0)
                pb = lens_v[b] - 1 - off
                s = _dot(qf.astype(BF16), k_v[l, b]) * dh ** -0.5
                sn = jnp.sum(qf * kn[r, bb:bb + 1, :], axis=1, keepdims=True) * dh ** -0.5
                s = jnp.where(col < pb, s, jnp.where(col == pb, sn, -jnp.inf))
                m = jnp.maximum(jnp.max(s, axis=1, keepdims=True), NEG)
                p = jnp.exp(s - m)
                den = jnp.sum(p, axis=1, keepdims=True)
                inside = jnp.logical_and(pb >= 0, pb < s_dev)
                pn = jnp.where(inside, jnp.exp(sn - m), 0.0)
                pz = jnp.where(col == pb, 0.0, p).astype(BF16)
                o = lax.dot_general(pz, v_v[l, b], (((1,), (1,)), ((), ())), preferred_element_type=F32)
                o = o + pn * vn[r, bb:bb + 1, :]
                for t in range(2):
                    te, to = slice(t * SUB, (t + 1) * SUB), slice(nc + t * SUB, nc + (t + 1) * SUB)
                    ev = o[te, t * LANES:(t + 1) * LANES]
                    od = o[to, t * LANES:(t + 1) * LANES]
                    evr = pltpu.roll(ev, dh, 1)
                    odr = pltpu.roll(od, dh, 1)
                    os[l, r, pl.ds(t * SUB * SUB + bb, SUB, stride=SUB), :] = jnp.where(
                        row < SUB // 2, jnp.where(lo, ev, odr), jnp.where(lo, evr, od))
                    for i, val in enumerate((m[te], den[te], m[to], den[to])):
                        stats[t] = jnp.where(lane == i * STW + bb, val, stats[t])
            for t in range(2):
                ss[l, r, t * SUB:(t + 1) * SUB, :] = stats[t]
            if l == 0 and r == 0:
                pl.semaphore_wait(bar, n - 1)
            to_owners([(lambda c: os.at[l, r, pl.ds(pl.multiple_of(c * SUB, SUB), SUB)], orv.at[l, r, me], sem(l, r, A2A)),
                       (lambda c: ss.at[l, r, pl.ds(c, 1)], sr.at[l, r, pl.ds(me, 1)], sem(l, r, STAT))])

        if l == 0:
            @pl.when(jnp.logical_not(own))
            def _():
                for c in wo_in:
                    c.start()

            @pl.when(own)
            def _():
                for c in wo_my:
                    c.start()
            for ll in range(1, nl):
                for c in ld[ll].values():
                    c.start()
        pad = jnp.zeros((LANES - nb, kvd), F32)
        knt[...] = jnp.concatenate([kn[0], kn[1], pad], axis=0).T
        vnt[...] = jnp.concatenate([vn[0], vn[1], pad], axis=0).T
        put_new(l, knt, k_v)

        @pl.when(own)
        def _():
            for r in range(2):
                orv[l, r, me] = os[l, r, pl.ds(pl.multiple_of(mc * SUB, SUB), SUB), :]
                sr[l, r, pl.ds(me, 1), :] = ss[l, r, pl.ds(mc, 1), :]
                wait(orv.at[l, r], n - 1, rsem.at[sem(l, r, A2A)])
                wait(sr.at[l, r], n - 1, rsem.at[sem(l, r, STAT)])
                sa = sr[l, r]
                w = jnp.exp(sa - jnp.max(sa, axis=0, keepdims=True))
                den = jnp.sum(w * pltpu.roll(sa, LANES - STW, 1), axis=0, keepdims=True)
                cf = jnp.concatenate([w / den, jnp.zeros((LANES - n, LANES), F32)], axis=0).T
                acc = jnp.zeros((SUB, LANES), F32)
                for i in range(n):
                    f = jnp.where(lo, cf[0:SUB, i:i + 1], cf[2 * STW:2 * STW + SUB, i:i + 1])
                    acc = acc + f * orv[l, r, i]
                if r == 0:
                    wo_in[l].wait_recv()
                    wo_my[l].wait()
                part = _dot(acc.astype(BF16), wo_v[l])
                for c in range(nc):
                    s1[l, r, c] = part[:, c * LANES:(c + 1) * LANES]

                def body(k, carry):
                    c = lax.rem(mc + k, nc)
                    rcopy(s1.at[l, r, c], r1.at[l, r, mc], sem(l, r, RS1), 2 * c + OWN).start()
                    return carry
                lax.fori_loop(1, nc, body, 0)
                r1[l, r, mc] = s1[l, r, mc]

        put_new(l, vnt, v_v)

        @pl.when(own)
        def _():
            for r in range(2):
                wait(r1.at[l, r], nc - 1, rsem.at[sem(l, r, RS1)])
                tot = r1[l, r, 0]
                for c in range(1, nc):
                    tot = tot + r1[l, r, c]
                gather(l, st, r, AG1, (hb[0, r, mc] if st == 0 else hs[st - 1, r]) + tot)

        for r in range(2):
            gathered(l, st, r, AG1)
            if r == 0:
                if l == 0:
                    ld[0]['g2'].wait()
                ld[l]['w1'].wait()
                ld[l]['w2'].wait()
            normed(st + 1, r, g2_v, l)
            u = jax.nn.gelu(_dot(xn[r], w1_v[l]), approximate=True).astype(BF16)
            part = _dot(u, w2_v[l])
            for c in range(nc):
                s2[l, r, c] = part[:, c * LANES:(c + 1) * LANES]
            to_owners([(lambda c: s2.at[l, r, c], r2.at[l, r, me], sem(l, r, RS2))])

        @pl.when(own)
        def _():
            for r in range(2):
                r2[l, r, me] = s2[l, r, mc]
                wait(r2.at[l, r], n - 1, rsem.at[sem(l, r, RS2)])
                tot = r2[l, r, 0]
                for d in range(1, n):
                    tot = tot + r2[l, r, d]
                gather(l, st + 1, r, AG2, hs[st, r] + tot)
        st += 2

    for r in range(2):
        gathered(nl - 1, st - 1, r, AG2)
    for c in range(nc):
        y_ref[:, c * LANES:(c + 1) * LANES] = jnp.concatenate([hb[st, 0, c], hb[st, 1, c]], axis=0).astype(BF16)

    @pl.when(own)
    def _():
        for l in range(nl):
            for r in range(2):
                wait(orv.at[l, r], nc - 1, ssem.at[sem(l, r, A2A)])
                wait(sr.at[l, r], nc - 1, ssem.at[sem(l, r, STAT)])
                wait(r1.at[l, r], nc - 1, ssem.at[sem(l, r, RS1)])
                wait(orv.at[l, r], n - 1, ssem.at[sem(l, r, AG1)])
                wait(r1.at[l, r], nc - 1, ssem.at[sem(l, r, RS2)])
                wait(orv.at[l, r], n - 1, ssem.at[sem(l, r, AG2)])

    @pl.when(jnp.logical_not(own))
    def _():
        for l in range(nl):
            wo_in[l].wait_send()
            for r in range(2):
                wait(orv.at[l, r], nc, ssem.at[sem(l, r, A2A)])
                wait(sr.at[l, r], nc, ssem.at[sem(l, r, STAT)])
                wait(r1.at[l, r], nc, ssem.at[sem(l, r, RS2)])


def _cache_kernel(y_ref, k_ref, v_ref, y_out, k_out, v_out, sem):
    cps = [pltpu.make_async_copy(s, d, sem.at[i])
           for i, (s, d) in enumerate(((y_ref, y_out), (k_ref, k_out), (v_ref, v_out)))]
    for c in cps:
        c.start()
    for c in cps:
        c.wait()


def solution(mesh):
    n = mesh.shape['sp']
    kspec = P(None, 'dp', 'sp', None, None)

    def local(x, lens, wq, wk, wv, wo, w1, w2, g1, g2, kc, vc):
        nl, nb, s_dev, kvh, dh = kc.shape
        D = x.shape[1]
        kvd = kvh * dh
        ff = w1.shape[2]
        nc = n // 2
        kt = jnp.transpose(kc, (0, 1, 3, 4, 2)).reshape(nl, nb, kvd, s_dev)
        vt = jnp.transpose(vc, (0, 1, 3, 4, 2)).reshape(nl, nb, kvd, s_dev)
        vm = pl.BlockSpec(memory_space=pltpu.VMEM)
        anys = pl.BlockSpec(memory_space=pl.ANY)
        tile = (SUB, LANES)
        y, ks, vs = pl.pallas_call(
            functools.partial(_step_kernel, n, (nl, nb, s_dev, kvd, dh)),
            out_shape=(pltpu.VMEM((nb, D), BF16), pltpu.VMEM(kt.shape, BF16), pltpu.VMEM(vt.shape, BF16)),
            in_specs=[anys] * 12,
            out_specs=(vm, vm, vm),
            scratch_shapes=[
                pltpu.VMEM((nl, D, D), BF16),
                pltpu.VMEM((nl, D, kvd), BF16),
                pltpu.VMEM((nl, D, kvd), BF16),
                pltpu.VMEM((nl, 2 * dh, D), BF16),
                pltpu.VMEM((nl, D, ff), BF16),
                pltpu.VMEM((nl, ff, D), BF16),
                pltpu.VMEM(x.shape, BF16),
                pltpu.VMEM(g1.shape, BF16),
                pltpu.VMEM(g2.shape, BF16),
                pltpu.SMEM(lens.shape, jnp.int32),
                pltpu.VMEM((2, SUB * nc, LANES), F32),
                pltpu.VMEM((2, SUB, kvd), F32),
                pltpu.VMEM((2, SUB, kvd), F32),
                pltpu.VMEM((kvd, LANES), F32),
                pltpu.VMEM((kvd, LANES), F32),
                pltpu.VMEM((2, SUB, D), BF16),
                pltpu.VMEM((2 * nl + 1, 2, nc) + tile, F32),
                pltpu.VMEM((2 * nl, 2) + tile, F32),
                pltpu.VMEM((nl, 2, nc * SUB, LANES), F32),
                pltpu.VMEM((nl, 2, n) + tile, F32),
                pltpu.VMEM((nl, 2, nc, LANES), F32),
                pltpu.VMEM((nl, 2, n, LANES), F32),
                pltpu.VMEM((nl, 2, nc) + tile, F32),
                pltpu.VMEM((nl, 2, nc) + tile, F32),
                pltpu.VMEM((nl, 2, nc) + tile, F32),
                pltpu.VMEM((nl, 2, n) + tile, F32),
                pltpu.SemaphoreType.DMA((nl, QCH + 13)),
                pltpu.SemaphoreType.DMA((14 * nl,)),
                pltpu.SemaphoreType.DMA((14 * nl,)),
            ],
            compiler_params=pltpu.CompilerParams(
                collective_id=0, has_side_effects=True, vmem_limit_bytes=40 * 1024 * 1024),
        )(lens, x, g1, g2, wq, wk, wv, wo, w1, w2, kt, vt)

        y, k2, v2 = pl.pallas_call(
            _cache_kernel,
            out_shape=(jax.ShapeDtypeStruct((nb, D), BF16), jax.ShapeDtypeStruct(kt.shape, BF16),
                       jax.ShapeDtypeStruct(vt.shape, BF16)),
            in_specs=[vm, vm, vm],
            out_specs=(anys, anys, anys),
            scratch_shapes=[pltpu.SemaphoreType.DMA((3,))],
            compiler_params=pltpu.CompilerParams(vmem_limit_bytes=1024 * 1024),
        )(y, ks, vs)

        def back(a):
            return jnp.transpose(a.reshape(nl, nb, kvh, dh, s_dev), (0, 1, 4, 2, 3))
        return y, back(k2), back(v2)

    return jax.shard_map(
        local, mesh=mesh,
        in_specs=(P('dp', None), P('dp'), P(), P(), P(), P(None, 'sp', None), P(None, None, 'sp'),
                  P(None, 'sp', None), P(), P(), kspec, kspec),
        out_specs=(P('dp', None), kspec, kspec), check_vma=False)
```

time: 710 us -> 75.7 us (0.11)
  waiting for transfers between devices: 439 us -> 0 us
  blocking collectives: 183 us -> 0 us
  Pallas kernels: 0 us -> 74.8 us
  matrix products: 37.2 us -> 0 us
  other arithmetic: 33.6 us -> 0 us
  between operations: 14.3 us -> 0.8 us
    psum x6 -> x0, waiting for transfers between devices: 438 us -> none  [the longest x2 173 us: local(): h = h + lax.psum(_mm(att, wo[l]), 'sp')]
    pmax x2 -> x0, blocking collectives: 95.7 us -> none  [local(): c = jnp.exp(m - lax.pmax(m, 'sp'))]
    psum x2 -> x0, blocking collectives: 87.7 us -> none  [local(): o, den = lax.psum((o * c[..., None], den * c), 'sp')]
    pallas_call x0 -> x2, Pallas kernels: none -> 74.8 us  [the longest x1 68.6 us: local(): pl.pallas_call(functools.partial(_step_kernel, n, (nl, nb, s_dev, kvd, dh...]
    dot_general x14 -> x0, matrix products: 37.2 us -> none  [the longest x10 23 us: _mm(): return jnp.dot(a, w, preferred_element_type=jnp.float32)]
    select_n x3 -> x0, other arithmetic: 11.8 us -> none  [the longest x1 11.8 us: local(): vl = jnp.where(write, v, vc[l])]
    another operation x1 -> x0, other arithmetic: 11.6 us -> none  [local(): return (h.astype(jnp.bfloat16), jnp.stack(ks), jnp.stack(vs))]
  transfers between devices with their start and end apart: 6 -> 0, of which waited for: 6 -> 0; matrix products, arithmetic and copies ran while one was open for 3% -> 0% of each run, Pallas kernels for 0% -> 0%
where the time goes in v2:
time: 75.7 us; the launch traced here: 75.6 us
  Pallas kernels  74.8 us (99%)
  between operations  0.8 us (1%)
    pallas_call x1, Pallas kernels, local(): pl.pallas_call(functools.partial(_step_kernel, n, (nl, nb, s_dev, kvd, dh...  68.6 us
    pallas_call x1, Pallas kernels, local(): pl.pallas_call(_cache_kernel, out_shape=(jax.ShapeDtypeStruct((nb, D), BF...  6.21 us

profile of v2, /device:TPU:97, one launch (start us, length us, event | category | flops | bytes accessed | tf_op | source)
XLA Modules:
  0.0 75.6 jit_solution(1550086922152474329)
XLA Ops:
  0.6 68.6 %shard_map.139 = (bf16[16,2048]{1,0:T(8,128)(2,1)S(1)}, bf16[2,16,256,512]{3,2,1,0:T(8,128)(2,1)S(1)}, bf16[2,16,256,512]{3,2,1,0:T(8,128)(2,1)S(1)}) custom-call(s32[16]{0:T(128)} %lens.1, bf16[16,2048]{1,0:T(8,128)(2,1)} %x.1, bf16[2,2048]{1,0:T(2,128)(2,1)} %g1.1, bf16[2,2048]{1,0:T(2,128)(2,1)} %g2.1, bf16[2,2048,2048]{2,1,0:T(8,128)(2,1)} %wq.1, ...), custom_call_target="tpu_custom_call" | custom-call | tf_op jit(solution)/shard_map/pallas_call | solution.py:354
  69.3 6.2 %shard_map.140 = (bf16[16,2048]{1,0:T(8,128)(2,1)}, bf16[2,16,256,512]{3,2,1,0:T(8,128)(2,1)}, bf16[2,16,256,512]{3,2,1,0:T(8,128)(2,1)}) custom-call(bf16[16,2048]{1,0:T(8,128)(2,1)S(1)} %get-tuple-element.9.y_ref, bf16[2,16,256,512]{3,2,1,0:T(8,128)(2,1)S(1)} %get-tuple-element.10.k_ref, bf16[2,16,256,512]{3,2,1,0:T(8,128)(2,1)S(1)} %get-tuple-element.11.v_ref), custom_call_target="tpu_custom_call" | custom-call | tf_op jit(solution)/shard_map/pallas_call | solution.py:394

commit v3 on v2

v3 whole, which is shorter than its diff:
```python
import functools

import jax
import jax.numpy as jnp
from jax import lax
from jax.experimental import pallas as pl
from jax.experimental.pallas import tpu as pltpu
from jax.sharding import PartitionSpec as P

EPS = 1e-6
LANES = 128
SUB = 8
NEG = float(jnp.finfo(jnp.float32).min)
F32 = jnp.float32
BF16 = jnp.bfloat16
MESH = pl.DeviceIdType.MESH
QCH = 4
OWN = 1
PIECES = 4
STW = 32


def _dot(a, w):
    return jnp.dot(a, w, preferred_element_type=F32)


def _step_kernel(n, dims, lens, x, g1, g2, wq, wk, wv, wo, w1, w2, kc, vc,
                 y_ref, k_v, v_v,
                 wq_v, wk_v, wv_v, wo_v, w1_v, w2_v, x_v, g1_v, g2_v, lens_v, sc, sns, pc, qs, kv, knt, vnt, xn, hb, hs,
                 ys, yb, os, orv, ss, sr, s1, r1, s2, r2, lsem, ssem, rsem):
    nl, nb, s_dev, kvd, dh = dims
    D = x_v.shape[1]
    nc = n // 2
    me = lax.axis_index('sp')
    par = lax.rem(me, 2)
    mc = lax.div(me, 2)
    own = par == OWN
    other = me + 1 - 2 * par

    cw = D // QCH
    hw = D // 2

    def local_copy(src, dst, l, i):
        return pltpu.make_async_copy(src, dst, lsem.at[l, i])

    hq = hw // QCH
    l_x = [local_copy(s, d, 0, i) for i, (s, d) in enumerate(((x, x_v), (g1, g1_v), (lens, lens_v), (g2, g2_v)))]
    l_k0 = local_copy(wk.at[0], wk_v.at[0], 0, 4)
    l_v0 = local_copy(wv.at[0], wk_v.at[0], 0, 4)
    l_q0 = []
    for j in range(QCH):
        sl = pl.ds(pl.multiple_of(par * hw + j * hq, LANES), hq)
        l_q0.append(local_copy(wq.at[0, :, sl], wq_v.at[0, :, pl.ds(j * hq, hq)], 0, 5 + j))
    l_q1 = [local_copy(wq.at[l, :, pl.ds(j * cw, cw)], wq_v.at[l, :, pl.ds(j * cw, cw)], l, 5 + j)
            for l in range(1, nl) for j in range(QCH)]
    l_q1 += [local_copy(wk.at[l], wk_v.at[l], l, 3) for l in range(1, nl)]
    l_q1 += [local_copy(wv.at[l], wv_v.at[l], l, 4) for l in range(1, nl)]
    o = 5 + QCH
    l_kv = [[[local_copy(a.at[l, pl.ds(r * SUB, SUB)], b.at[l, pl.ds(r * SUB, SUB)], l, o + 2 * r + i)
              for i, (a, b) in enumerate(((kc, k_v), (vc, v_v)))] for r in range(2)] for l in range(nl)]
    l_w = [[local_copy(w1.at[l], w1_v.at[l], l, o + 4), local_copy(w2.at[l], w2_v.at[l], l, o + 5)] for l in range(nl)]

    def start(cs):
        for c in cs:
            c.start()

    def done(cs):
        for c in cs:
            c.wait()

    start(l_x[:3])

    @pl.when(par == 0)
    def _():
        l_k0.start()

    @pl.when(par == 1)
    def _():
        l_v0.start()
    start(l_q0)

    bar = pltpu.get_barrier_semaphore()

    def sig(k, carry):
        pl.semaphore_signal(bar, 1, device_id={'sp': lax.rem(me + k, n)}, device_id_type=MESH)
        return carry
    lax.fori_loop(1, n, sig, 0)

    A2A, STAT, RS1, AG1, RS2, AG2, WO, XQ, XKV = range(9)

    def sem(l, r, kind):
        return (l * 2 + r) * 9 + kind

    def rcopy(src, dst, i, d):
        return pltpu.make_async_remote_copy(src, dst, ssem.at[i], rsem.at[i], device_id={'sp': d}, device_id_type=MESH)

    def to_owners(pairs):
        def body(k, carry):
            c = lax.rem(mc + k, nc)
            for src, dst, i in pairs:
                rcopy(src(c), dst, i, 2 * c + OWN).start()
            return carry
        lax.fori_loop(1, nc, body, 0)

        @pl.when(jnp.logical_not(own))
        def _():
            body(0, 0)

    def wait(ref, count, s):
        r = ref.at[pl.ds(0, count)]
        pltpu.make_async_copy(r, r, s).wait()

    lane = lax.broadcasted_iota(jnp.int32, (SUB, LANES), 1)
    row = lax.broadcasted_iota(jnp.int32, (SUB, LANES), 0)
    lo = lane < dh
    ma = (row < SUB // 2) & lo
    mb = (row >= SUB // 2) & (~lo)
    col = lax.broadcasted_iota(jnp.int32, (2 * nc, s_dev), 1)
    col1 = lax.broadcasted_iota(jnp.int32, (1, s_dev), 1)
    off = me * s_dev

    def normed(st, r, g_v, l):
        ss_ = None
        for c in range(nc):
            t = hb[st, r, c]
            ss_ = t * t if ss_ is None else ss_ + t * t
        rr = lax.rsqrt(jnp.sum(ss_, axis=1, keepdims=True) / D + EPS)
        for c in range(nc):
            g = g_v[l:l + 1, c * LANES:(c + 1) * LANES].astype(F32)
            xn[r * SUB:(r + 1) * SUB, c * LANES:(c + 1) * LANES] = (hb[st, r, c] * rr * g).astype(BF16)

    def gather(l, st, r, kind, h):
        if st == 2 * nl - 1:
            ys[r] = h.astype(BF16)
            src, dst = ys.at[r], yb
        else:
            hs[st, r] = h
            src, dst = hs.at[st, r], hb.at[st + 1]

        def body(k, carry):
            rcopy(src, dst.at[r, mc], sem(l, r, kind), lax.rem(me + k, n)).start()
            return carry
        lax.fori_loop(1, n, body, 0)
        dst[r, mc] = src[...]

    def gathered(l, st, r, kind):
        dst = yb if st == 2 * nl - 1 else hb.at[st + 1]

        @pl.when(own)
        def _():
            wait(dst.at[r], nc - 1, rsem.at[sem(l, r, kind)])

        @pl.when(jnp.logical_not(own))
        def _():
            wait(dst.at[r], nc, rsem.at[sem(l, r, kind)])

    def put_new(l, new_t, ref):
        for b in range(nb):
            pb = lens_v[b] - 1 - off
            hit = jnp.where(col1 == pb, 1.0, 0.0).astype(BF16)
            c = jnp.broadcast_to(new_t[:, b:b + 1], (kvd, LANES)).astype(BF16)
            for t in range(s_dev // LANES):
                sl = slice(t * LANES, (t + 1) * LANES)
                hm = jnp.broadcast_to(hit[:, sl], (kvd, LANES)) > 0.5
                ref[l, b, :, sl] = jnp.where(hm, c, ref[l, b, :, sl])

    def store_q(half, rs, c0, q):
        q = q.astype(BF16).astype(F32)
        for t in range(q.shape[1] // LANES):
            for i, r in enumerate(rs):
                qs[half, r, pl.ds(c0 + t, SUB, stride=SUB), :] = q[i * SUB:(i + 1) * SUB, t * LANES:(t + 1) * LANES]

    def store_kv(i, rs, a):
        kv[i, rs] = a.astype(BF16).astype(F32).reshape(-1, SUB, kvd)

    def qkv(l, r):
        a = xn[r * SUB:(r + 1) * SUB, :]
        store_kv(0, slice(r, r + 1), _dot(a, wk_v[l]))
        store_kv(1, slice(r, r + 1), _dot(a, wv_v[l]))
        for j in range(QCH):
            q = _dot(a, wq_v[l, :, j * cw:(j + 1) * cw])
            store_q(j * cw // hw, (r,), j * (cw // LANES) % SUB, q)

    def scores(l, r):
        z = jnp.zeros((SUB, LANES), F32)
        for bb in range(SUB):
            xq = jnp.concatenate([qs[i, r, bb * SUB:(bb + 1) * SUB, :] for i in range(2)], axis=0)
            xr = pltpu.roll(xq, dh, 1)
            parts = []
            for a, o in ((xq, xr), (xr, xq)):
                e0 = jnp.where(ma, a[0:SUB], jnp.where(mb, o[0:SUB], 0.0))
                e1 = jnp.where(ma, a[SUB:], jnp.where(mb, o[SUB:], 0.0))
                parts.append(jnp.concatenate([e0, z], axis=1))
                parts.append(jnp.concatenate([z, e1], axis=1))
            qf = jnp.concatenate(parts, axis=0)
            sc[r, bb] = _dot(qf.astype(BF16), k_v[l, r * SUB + bb])
            sn = jnp.sum(qf * kv[0, r, bb:bb + 1, :], axis=1, keepdims=True) * dh ** -0.5
            sns[r, bb] = jnp.broadcast_to(sn, (2 * nc, LANES))

    def probs(l, r):
        stats = [jnp.zeros((SUB, LANES), F32) for _ in range(2)]
        for bb in range(SUB):
            pb = lens_v[r * SUB + bb] - 1 - off
            sn = sns[r, bb]
            sn4 = jnp.concatenate([sn] * (s_dev // LANES), axis=1)
            s = sc[r, bb] * dh ** -0.5
            s = jnp.where(col < pb, s, jnp.where(col == pb, sn4, -jnp.inf))
            m = jnp.maximum(jnp.max(s, axis=1, keepdims=True), NEG)
            p = jnp.exp(s - m)
            den = jnp.sum(p, axis=1, keepdims=True)
            inside = jnp.logical_and(pb >= 0, pb < s_dev)
            sns[r, bb] = jnp.where(inside, jnp.exp(sn - m), 0.0)
            pc[r, bb] = jnp.where(col == pb, 0.0, p).astype(BF16)
            for t in range(2):
                te, to = slice(t * SUB, (t + 1) * SUB), slice(nc + t * SUB, nc + (t + 1) * SUB)
                for i, val in enumerate((m[te], den[te], m[to], den[to])):
                    stats[t] = jnp.where(lane == i * STW + bb, val, stats[t])
        for t in range(2):
            ss[l, r, t * SUB:(t + 1) * SUB, :] = stats[t]

    def values(l, r):
        for bb in range(SUB):
            o = lax.dot_general(pc[r, bb], v_v[l, r * SUB + bb], (((1,), (1,)), ((), ())), preferred_element_type=F32)
            pn = sns[r, bb]
            o = o + jnp.concatenate([pn] * (kvd // LANES), axis=1) * kv[1, r, bb:bb + 1, :]
            for t in range(2):
                ev = o[t * SUB:(t + 1) * SUB, t * LANES:(t + 1) * LANES]
                od = o[nc + t * SUB:nc + (t + 1) * SUB, t * LANES:(t + 1) * LANES]
                evr = pltpu.roll(ev, dh, 1)
                odr = pltpu.roll(od, dh, 1)
                os[l, r, pl.ds(t * SUB * SUB + bb, SUB, stride=SUB), :] = jnp.where(
                    row < SUB // 2, jnp.where(lo, ev, odr), jnp.where(lo, evr, od))

    def send_partials(l, r):
        to_owners([(lambda c: os.at[l, r, pl.ds(pl.multiple_of(c * SUB, SUB), SUB)], orv.at[l, r, me], sem(l, r, A2A)),
                   (lambda c: ss.at[l, r, pl.ds(c, 1)], sr.at[l, r, pl.ds(me, 1)], sem(l, r, STAT))])

    done(l_x[:2])
    for c in range(nc):
        for r in range(2):
            hb[0, r, c] = x_v[r * SUB:(r + 1) * SUB, c * LANES:(c + 1) * LANES].astype(F32)

    wo_in = [rcopy(wo.at[ll], wo_v.at[ll, pl.ds((1 - OWN) * dh, dh)], sem(ll, 0, WO), other) for ll in range(nl)]
    wo_my = [pltpu.make_async_copy(wo.at[ll], wo_v.at[ll, pl.ds(OWN * dh, dh)], lsem.at[ll, QCH + 11])
             for ll in range(nl)]
    st = 0
    for l in range(nl):
        if l == 0:
            for r in range(2):
                normed(st, r, g1_v, l)
            l_k0.wait()
            store_kv(par, slice(None), _dot(xn[...], wk_v[0]))
            for j in range(QCH):
                l_q0[j].wait()
                if j == 1:
                    start(l_kv[0][0])
                q = _dot(xn[...], wq_v[0, :, j * hq:(j + 1) * hq])
                store_q(par, (0, 1), j * (hq // LANES), q)
            start(l_kv[0][1])
            pl.semaphore_wait(bar, n - 1)
            swap = [rcopy(b.at[par], b.at[par], sem(0, 0, i), other) for b, i in ((qs, XQ), (kv, XKV))]
            start(swap)
            l_x[2].wait()
            for c in swap:
                c.wait_recv()
            done(l_kv[0][0])
            scores(l, 0)
            done(l_kv[0][1])
            start(l_x[3:])
            start(l_w[0])
            probs(l, 0)
            scores(l, 1)
        else:
            gathered(l - 1, st - 1, 0, AG2)
            normed(st, 0, g1_v, l)
            done(l_q1)
            qkv(l, 0)
            done(l_kv[l][0])
            scores(l, 0)
            gathered(l - 1, st - 1, 1, AG2)
            normed(st, 1, g1_v, l)
            probs(l, 0)
            qkv(l, 1)
        values(l, 0)
        send_partials(l, 0)
        if l > 0:
            done(l_kv[l][1])
            scores(l, 1)
        probs(l, 1)
        values(l, 1)
        send_partials(l, 1)
        if l == 0:
            for c in swap:
                c.wait_send()

        if l == 0:
            @pl.when(jnp.logical_not(own))
            def _():
                for c in wo_in:
                    c.start()

            @pl.when(own)
            def _():
                for c in wo_my:
                    c.start()
            start(l_q1)
            for ll in range(1, nl):
                start(l_kv[ll][0] + l_kv[ll][1] + l_w[ll])
        pad = jnp.zeros((LANES - nb, kvd), F32)
        knt[...] = jnp.concatenate([kv[0, 0], kv[0, 1], pad], axis=0).T
        vnt[...] = jnp.concatenate([kv[1, 0], kv[1, 1], pad], axis=0).T
        put_new(l, knt, k_v)

        @pl.when(own)
        def _():
            for r in range(2):
                orv[l, r, me] = os[l, r, pl.ds(pl.multiple_of(mc * SUB, SUB), SUB), :]
                sr[l, r, pl.ds(me, 1), :] = ss[l, r, pl.ds(mc, 1), :]
                wait(orv.at[l, r], n - 1, rsem.at[sem(l, r, A2A)])
                wait(sr.at[l, r], n - 1, rsem.at[sem(l, r, STAT)])
                sa = sr[l, r]
                w = jnp.exp(sa - jnp.max(sa, axis=0, keepdims=True))
                den = jnp.sum(w * pltpu.roll(sa, LANES - STW, 1), axis=0, keepdims=True)
                cf = jnp.concatenate([w / den, jnp.zeros((LANES - n, LANES), F32)], axis=0).T
                acc = jnp.zeros((SUB, LANES), F32)
                for i in range(n):
                    f = jnp.where(lo, cf[0:SUB, i:i + 1], cf[2 * STW:2 * STW + SUB, i:i + 1])
                    acc = acc + f * orv[l, r, i]
                if r == 0:
                    wo_in[l].wait_recv()
                    wo_my[l].wait()
                part = _dot(acc.astype(BF16), wo_v[l])
                for c in range(nc):
                    s1[l, r, c] = part[:, c * LANES:(c + 1) * LANES]

                def body(k, carry):
                    c = lax.rem(mc + k, nc)
                    rcopy(s1.at[l, r, c], r1.at[l, r, mc], sem(l, r, RS1), 2 * c + OWN).start()
                    return carry
                lax.fori_loop(1, nc, body, 0)
                r1[l, r, mc] = s1[l, r, mc]

        put_new(l, vnt, v_v)

        @pl.when(own)
        def _():
            for r in range(2):
                wait(r1.at[l, r], nc - 1, rsem.at[sem(l, r, RS1)])
                tot = r1[l, r, 0]
                for c in range(1, nc):
                    tot = tot + r1[l, r, c]
                gather(l, st, r, AG1, (hb[0, r, mc] if st == 0 else hs[st - 1, r]) + tot)

        for r in range(2):
            gathered(l, st, r, AG1)
            if r == 0:
                if l == 0:
                    done(l_x[3:])
                done(l_w[l])
            normed(st + 1, r, g2_v, l)
            u = jax.nn.gelu(_dot(xn[r * SUB:(r + 1) * SUB, :], w1_v[l]), approximate=True).astype(BF16)
            part = _dot(u, w2_v[l])
            for c in range(nc):
                s2[l, r, c] = part[:, c * LANES:(c + 1) * LANES]
            to_owners([(lambda c: s2.at[l, r, c], r2.at[l, r, me], sem(l, r, RS2))])

        @pl.when(own)
        def _():
            for r in range(2):
                r2[l, r, me] = s2[l, r, mc]
                wait(r2.at[l, r], n - 1, rsem.at[sem(l, r, RS2)])
                tot = r2[l, r, 0]
                for d in range(1, n):
                    tot = tot + r2[l, r, d]
                gather(l, st + 1, r, AG2, hs[st, r] + tot)
        st += 2

    for r in range(2):
        gathered(nl - 1, st - 1, r, AG2)
    for c in range(nc):
        y_ref[:, c * LANES:(c + 1) * LANES] = jnp.concatenate([yb[0, c], yb[1, c]], axis=0)

    @pl.when(own)
    def _():
        for l in range(nl):
            for r in range(2):
                wait(orv.at[l, r], nc - 1, ssem.at[sem(l, r, A2A)])
                wait(sr.at[l, r], nc - 1, ssem.at[sem(l, r, STAT)])
                wait(r1.at[l, r], nc - 1, ssem.at[sem(l, r, RS1)])
                wait(orv.at[l, r], n - 1, ssem.at[sem(l, r, AG1)])
                wait(r1.at[l, r], nc - 1, ssem.at[sem(l, r, RS2)])
                wait(yb.at[r] if l == nl - 1 else orv.at[l, r], n - 1, ssem.at[sem(l, r, AG2)])

    @pl.when(jnp.logical_not(own))
    def _():
        for l in range(nl):
            wo_in[l].wait_send()
            for r in range(2):
                wait(orv.at[l, r], nc, ssem.at[sem(l, r, A2A)])
                wait(sr.at[l, r], nc, ssem.at[sem(l, r, STAT)])
                wait(r1.at[l, r], nc, ssem.at[sem(l, r, RS2)])


def _cache_kernel(y_ref, k_ref, v_ref, y_out, k_out, v_out, sem):
    cps = [pltpu.make_async_copy(y_ref, y_out, sem.at[0])]
    for a, b in ((k_ref, k_out), (v_ref, v_out)):
        for l in range(a.shape[0]):
            for i in range(PIECES):
                sl = pl.ds(i * (a.shape[1] // PIECES), a.shape[1] // PIECES)
                cps.append(pltpu.make_async_copy(a.at[l, sl], b.at[l, sl], sem.at[len(cps)]))
    for c in cps:
        c.start()
    for c in cps:
        c.wait()


def solution(mesh):
    n = mesh.shape['sp']
    kspec = P(None, 'dp', 'sp', None, None)

    def local(x, lens, wq, wk, wv, wo, w1, w2, g1, g2, kc, vc):
        nl, nb, s_dev, kvh, dh = kc.shape
        D = x.shape[1]
        kvd = kvh * dh
        ff = w1.shape[2]
        nc = n // 2
        kt = jnp.transpose(kc, (0, 1, 3, 4, 2)).reshape(nl, nb, kvd, s_dev)
        vt = jnp.transpose(vc, (0, 1, 3, 4, 2)).reshape(nl, nb, kvd, s_dev)
        vm = pl.BlockSpec(memory_space=pltpu.VMEM)
        anys = pl.BlockSpec(memory_space=pl.ANY)
        tile = (SUB, LANES)
        y, ks, vs = pl.pallas_call(
            functools.partial(_step_kernel, n, (nl, nb, s_dev, kvd, dh)),
            out_shape=(pltpu.VMEM((nb, D), BF16), pltpu.VMEM(kt.shape, BF16), pltpu.VMEM(vt.shape, BF16)),
            in_specs=[anys] * 12,
            out_specs=(vm, vm, vm),
            scratch_shapes=[
                pltpu.VMEM((nl, D, D), BF16),
                pltpu.VMEM((nl, D, kvd), BF16),
                pltpu.VMEM((nl, D, kvd), BF16),
                pltpu.VMEM((nl, 2 * dh, D), BF16),
                pltpu.VMEM((nl, D, ff), BF16),
                pltpu.VMEM((nl, ff, D), BF16),
                pltpu.VMEM(x.shape, BF16),
                pltpu.VMEM(g1.shape, BF16),
                pltpu.VMEM(g2.shape, BF16),
                pltpu.SMEM(lens.shape, jnp.int32),
                pltpu.VMEM((2, SUB, 2 * nc, s_dev), F32),
                pltpu.VMEM((2, SUB, 2 * nc, LANES), F32),
                pltpu.VMEM((2, SUB, 2 * nc, s_dev), BF16),
                pltpu.VMEM((2, 2, SUB * nc // 2, LANES), F32),
                pltpu.VMEM((2, 2, SUB, kvd), F32),
                pltpu.VMEM((kvd, LANES), F32),
                pltpu.VMEM((kvd, LANES), F32),
                pltpu.VMEM((nb, D), BF16),
                pltpu.VMEM((2 * nl, 2, nc) + tile, F32),
                pltpu.VMEM((2 * nl - 1, 2) + tile, F32),
                pltpu.VMEM((2,) + tile, BF16),
                pltpu.VMEM((2, n) + tile, BF16),
                pltpu.VMEM((nl, 2, nc * SUB, LANES), F32),
                pltpu.VMEM((nl, 2, n) + tile, F32),
                pltpu.VMEM((nl, 2, nc, LANES), F32),
                pltpu.VMEM((nl, 2, n, LANES), F32),
                pltpu.VMEM((nl, 2, nc) + tile, F32),
                pltpu.VMEM((nl, 2, nc) + tile, F32),
                pltpu.VMEM((nl, 2, nc) + tile, F32),
                pltpu.VMEM((nl, 2, n) + tile, F32),
                pltpu.SemaphoreType.DMA((nl, QCH + 12)),
                pltpu.SemaphoreType.DMA((18 * nl,)),
                pltpu.SemaphoreType.DMA((18 * nl,)),
            ],
            compiler_params=pltpu.CompilerParams(
                collective_id=0, has_side_effects=True, vmem_limit_bytes=40 * 1024 * 1024),
        )(lens, x, g1, g2, wq, wk, wv, wo, w1, w2, kt, vt)

        y, k2, v2 = pl.pallas_call(
            _cache_kernel,
            out_shape=(jax.ShapeDtypeStruct((nb, D), BF16), jax.ShapeDtypeStruct(kt.shape, BF16),
                       jax.ShapeDtypeStruct(vt.shape, BF16)),
            in_specs=[vm, vm, vm],
            out_specs=(anys, anys, anys),
            scratch_shapes=[pltpu.SemaphoreType.DMA((1 + 2 * nl * PIECES,))],
            compiler_params=pltpu.CompilerParams(vmem_limit_bytes=1024 * 1024),
        )(y, ks, vs)

        def back(a):
            return jnp.transpose(a.reshape(nl, nb, kvh, dh, s_dev), (0, 1, 4, 2, 3))
        return y, back(k2), back(v2)

    return jax.shard_map(
        local, mesh=mesh,
        in_specs=(P('dp', None), P('dp'), P(), P(), P(), P(None, 'sp', None), P(None, None, 'sp'),
                  P(None, 'sp', None), P(), P(), kspec, kspec),
        out_specs=(P('dp', None), kspec, kspec), check_vma=False)
```

time: 75.7 us -> 72 us (0.951)
  Pallas kernels: 74.8 us -> 71.2 us
    pallas_call x1, Pallas kernels: 68.6 us -> 65.2 us  [local(): pl.pallas_call(functools.partial(_step_kernel, n, (nl, nb, s_dev, kvd, dh...]
where the time goes in v3:
time: 72 us; the launch traced here: 71.9 us
  Pallas kernels  71.2 us (99%)
    pallas_call x1, Pallas kernels, local(): pl.pallas_call(functools.partial(_step_kernel, n, (nl, nb, s_dev, kvd, dh...  65.2 us
    pallas_call x1, Pallas kernels, local(): pl.pallas_call(_cache_kernel, out_shape=(jax.ShapeDtypeStruct((nb, D), BF...  5.99 us

profile of v3, /device:TPU:97, one launch (start us, length us, event | category | flops | bytes accessed | tf_op | source)
XLA Modules:
  0.0 71.9 jit_solution(210387572496618465)
XLA Ops:
  0.6 65.2 %shard_map.139 = (bf16[16,2048]{1,0:T(8,128)(2,1)S(1)}, bf16[2,16,256,512]{3,2,1,0:T(8,128)(2,1)S(1)}, bf16[2,16,256,512]{3,2,1,0:T(8,128)(2,1)S(1)}) custom-call(s32[16]{0:T(128)} %lens.1, bf16[16,2048]{1,0:T(8,128)(2,1)} %x.1, bf16[2,2048]{1,0:T(2,128)(2,1)} %g1.1, bf16[2,2048]{1,0:T(2,128)(2,1)} %g2.1, bf16[2,2048,2048]{2,1,0:T(8,128)(2,1)} %wq.1, ...), custom_call_target="tpu_custom_call" | custom-call | tf_op jit(solution)/shard_map/pallas_call | solution.py:432
  65.9 6.0 %shard_map.140 = (bf16[16,2048]{1,0:T(8,128)(2,1)}, bf16[2,16,256,512]{3,2,1,0:T(8,128)(2,1)}, bf16[2,16,256,512]{3,2,1,0:T(8,128)(2,1)}) custom-call(bf16[16,2048]{1,0:T(8,128)(2,1)S(1)} %get-tuple-element.9.y_ref, bf16[2,16,256,512]{3,2,1,0:T(8,128)(2,1)S(1)} %get-tuple-element.10.k_ref, bf16[2,16,256,512]{3,2,1,0:T(8,128)(2,1)S(1)} %get-tuple-element.11.v_ref), custom_call_target="tpu_custom_call" | custom-call | tf_op jit(solution)/shard_map/pallas_call | solution.py:476

commit v4 on v3

--- a/solution.py
+++ b/solution.py
@@ -1,4 +1,5 @@
 import functools
+import math
 
 import jax
 import jax.numpy as jnp
@@ -16,8 +17,18 @@
 MESH = pl.DeviceIdType.MESH
 QCH = 4
 OWN = 1
-PIECES = 4
+PIECES = 2
 STW = 32
+
+
+def far_first(m):
+    core = 1 if m % 4 == 0 and math.isqrt(m) ** 2 == m else 2
+    side = math.isqrt(m // core)
+
+    def hops(k):
+        y, x = divmod(k // core, side)
+        return min(y, side - y) + min(x, side - x)
+    return sorted(range(1, m), key=lambda k: -hops(k))
 
 
 def _dot(a, w):
@@ -100,7 +111,8 @@
             for src, dst, i in pairs:
                 rcopy(src(c), dst, i, 2 * c + OWN).start()
             return carry
-        lax.fori_loop(1, nc, body, 0)
+        for k in far_first(nc):
+            body(k, 0)
 
         @pl.when(jnp.logical_not(own))
         def _():
@@ -140,7 +152,8 @@
         def body(k, carry):
             rcopy(src, dst.at[r, mc], sem(l, r, kind), lax.rem(me + k, n)).start()
             return carry
-        lax.fori_loop(1, n, body, 0)
+        for k in far_first(n):
+            body(k, 0)
         dst[r, mc] = src[...]
 
     def gathered(l, st, r, kind):
@@ -337,7 +350,8 @@
                     c = lax.rem(mc + k, nc)
                     rcopy(s1.at[l, r, c], r1.at[l, r, mc], sem(l, r, RS1), 2 * c + OWN).start()
                     return carry
-                lax.fori_loop(1, nc, body, 0)
+                for k in far_first(nc):
+                    body(k, 0)
                 r1[l, r, mc] = s1[l, r, mc]
 
         put_new(l, vnt, v_v)

time: 72 us -> 71.2 us (0.989)
  Pallas kernels: 71.2 us -> 70.3 us
    pallas_call x1, Pallas kernels: 65.2 us -> 64.4 us  [local(): pl.pallas_call(functools.partial(_step_kernel, n, (nl, nb, s_dev, kvd, dh...]
where the time goes in v4:
time: 71.2 us; the launch traced here: 71.1 us
  Pallas kernels  70.3 us (99%)
  between operations  0.8 us (1%)
    pallas_call x1, Pallas kernels, local(): pl.pallas_call(functools.partial(_step_kernel, n, (nl, nb, s_dev, kvd, dh...  64.4 us
    pallas_call x1, Pallas kernels, local(): pl.pallas_call(_cache_kernel, out_shape=(jax.ShapeDtypeStruct((nb, D), BF...  5.95 us

profile of v4, /device:TPU:97, one launch (start us, length us, event | category | flops | bytes accessed | tf_op | source)
XLA Modules:
  0.0 71.1 jit_solution(11554573734522062913)
XLA Ops:
  0.6 64.4 %shard_map.139 = (bf16[16,2048]{1,0:T(8,128)(2,1)S(1)}, bf16[2,16,256,512]{3,2,1,0:T(8,128)(2,1)S(1)}, bf16[2,16,256,512]{3,2,1,0:T(8,128)(2,1)S(1)}) custom-call(s32[16]{0:T(128)} %lens.1, bf16[16,2048]{1,0:T(8,128)(2,1)} %x.1, bf16[2,2048]{1,0:T(2,128)(2,1)} %g1.1, bf16[2,2048]{1,0:T(2,128)(2,1)} %g2.1, bf16[2,2048,2048]{2,1,0:T(8,128)(2,1)} %wq.1, ...), custom_call_target="tpu_custom_call" | custom-call | tf_op jit(solution)/shard_map/pallas_call | solution.py:446
  65.0 6.0 %shard_map.140 = (bf16[16,2048]{1,0:T(8,128)(2,1)}, bf16[2,16,256,512]{3,2,1,0:T(8,128)(2,1)}, bf16[2,16,256,512]{3,2,1,0:T(8,128)(2,1)}) custom-call(bf16[16,2048]{1,0:T(8,128)(2,1)S(1)} %get-tuple-element.9.y_ref, bf16[2,16,256,512]{3,2,1,0:T(8,128)(2,1)S(1)} %get-tuple-element.10.k_ref, bf16[2,16,256,512]{3,2,1,0:T(8,128)(2,1)S(1)} %get-tuple-element.11.v_ref), custom_call_target="tpu_custom_call" | custom-call | tf_op jit(solution)/shard_map/pallas_call | solution.py:490

commit v5 on v4

--- a/solution.py
+++ b/solution.py
@@ -18,6 +18,7 @@
 QCH = 4
 OWN = 1
 PIECES = 2
+MSG = 2 * SUB
 STW = 32
 
 
@@ -38,7 +39,7 @@
 def _step_kernel(n, dims, lens, x, g1, g2, wq, wk, wv, wo, w1, w2, kc, vc,
                  y_ref, k_v, v_v,
                  wq_v, wk_v, wv_v, wo_v, w1_v, w2_v, x_v, g1_v, g2_v, lens_v, sc, sns, pc, qs, kv, knt, vnt, xn, hb, hs,
-                 ys, yb, os, orv, ss, sr, s1, r1, s2, r2, lsem, ssem, rsem):
+                 ys, yb, os, orv, s1, r1, s2, r2, lsem, ssem, rsem):
     nl, nb, s_dev, kvd, dh = dims
     D = x_v.shape[1]
     nc = n // 2
@@ -189,10 +190,10 @@
     def qkv(l, r):
         a = xn[r * SUB:(r + 1) * SUB, :]
         store_kv(0, slice(r, r + 1), _dot(a, wk_v[l]))
-        store_kv(1, slice(r, r + 1), _dot(a, wv_v[l]))
         for j in range(QCH):
             q = _dot(a, wq_v[l, :, j * cw:(j + 1) * cw])
             store_q(j * cw // hw, (r,), j * (cw // LANES) % SUB, q)
+        store_kv(1, slice(r, r + 1), _dot(a, wv_v[l]))
 
     def scores(l, r):
         z = jnp.zeros((SUB, LANES), F32)
@@ -229,7 +230,7 @@
                 for i, val in enumerate((m[te], den[te], m[to], den[to])):
                     stats[t] = jnp.where(lane == i * STW + bb, val, stats[t])
         for t in range(2):
-            ss[l, r, t * SUB:(t + 1) * SUB, :] = stats[t]
+            os[l, r, pl.ds(t * SUB * MSG + SUB, SUB, stride=MSG), :] = stats[t]
 
     def values(l, r):
         for bb in range(SUB):
@@ -241,12 +242,12 @@
                 od = o[nc + t * SUB:nc + (t + 1) * SUB, t * LANES:(t + 1) * LANES]
                 evr = pltpu.roll(ev, dh, 1)
                 odr = pltpu.roll(od, dh, 1)
-                os[l, r, pl.ds(t * SUB * SUB + bb, SUB, stride=SUB), :] = jnp.where(
+                os[l, r, pl.ds(t * SUB * MSG + bb, SUB, stride=MSG), :] = jnp.where(
                     row < SUB // 2, jnp.where(lo, ev, odr), jnp.where(lo, evr, od))
 
     def send_partials(l, r):
-        to_owners([(lambda c: os.at[l, r, pl.ds(pl.multiple_of(c * SUB, SUB), SUB)], orv.at[l, r, me], sem(l, r, A2A)),
-                   (lambda c: ss.at[l, r, pl.ds(c, 1)], sr.at[l, r, pl.ds(me, 1)], sem(l, r, STAT))])
+        to_owners([(lambda c: os.at[l, r, pl.ds(pl.multiple_of(c * MSG, MSG), SUB + 1)],
+                    orv.at[l, r, pl.ds(pl.multiple_of(me * MSG, MSG), SUB + 1)], sem(l, r, A2A))])
 
     done(l_x[:2])
     for c in range(nc):
@@ -327,18 +328,18 @@
         @pl.when(own)
         def _():
             for r in range(2):
-                orv[l, r, me] = os[l, r, pl.ds(pl.multiple_of(mc * SUB, SUB), SUB), :]
-                sr[l, r, pl.ds(me, 1), :] = ss[l, r, pl.ds(mc, 1), :]
-                wait(orv.at[l, r], n - 1, rsem.at[sem(l, r, A2A)])
-                wait(sr.at[l, r], n - 1, rsem.at[sem(l, r, STAT)])
-                sa = sr[l, r]
+                for o, k in ((0, SUB), (SUB, 1)):
+                    orv[l, r, pl.ds(pl.multiple_of(me * MSG, MSG) + o, k), :] = os[
+                        l, r, pl.ds(pl.multiple_of(mc * MSG, MSG) + o, k), :]
+                wait(orv.at[l, r], (n - 1) * (SUB + 1), rsem.at[sem(l, r, A2A)])
+                sa = orv[l, r, pl.ds(SUB, n, stride=MSG), :]
                 w = jnp.exp(sa - jnp.max(sa, axis=0, keepdims=True))
                 den = jnp.sum(w * pltpu.roll(sa, LANES - STW, 1), axis=0, keepdims=True)
                 cf = jnp.concatenate([w / den, jnp.zeros((LANES - n, LANES), F32)], axis=0).T
                 acc = jnp.zeros((SUB, LANES), F32)
                 for i in range(n):
                     f = jnp.where(lo, cf[0:SUB, i:i + 1], cf[2 * STW:2 * STW + SUB, i:i + 1])
-                    acc = acc + f * orv[l, r, i]
+                    acc = acc + f * orv[l, r, i * MSG:i * MSG + SUB, :]
                 if r == 0:
                     wo_in[l].wait_recv()
                     wo_my[l].wait()
@@ -398,20 +399,18 @@
     def _():
         for l in range(nl):
             for r in range(2):
-                wait(orv.at[l, r], nc - 1, ssem.at[sem(l, r, A2A)])
-                wait(sr.at[l, r], nc - 1, ssem.at[sem(l, r, STAT)])
+                wait(orv.at[l, r], (nc - 1) * (SUB + 1), ssem.at[sem(l, r, A2A)])
                 wait(r1.at[l, r], nc - 1, ssem.at[sem(l, r, RS1)])
-                wait(orv.at[l, r], n - 1, ssem.at[sem(l, r, AG1)])
+                wait(r2.at[l, r], n - 1, ssem.at[sem(l, r, AG1)])
                 wait(r1.at[l, r], nc - 1, ssem.at[sem(l, r, RS2)])
-                wait(yb.at[r] if l == nl - 1 else orv.at[l, r], n - 1, ssem.at[sem(l, r, AG2)])
+                wait(yb.at[r] if l == nl - 1 else r2.at[l, r], n - 1, ssem.at[sem(l, r, AG2)])
 
     @pl.when(jnp.logical_not(own))
     def _():
         for l in range(nl):
             wo_in[l].wait_send()
             for r in range(2):
-                wait(orv.at[l, r], nc, ssem.at[sem(l, r, A2A)])
-                wait(sr.at[l, r], nc, ssem.at[sem(l, r, STAT)])
+                wait(orv.at[l, r], nc * (SUB + 1), ssem.at[sem(l, r, A2A)])
                 wait(r1.at[l, r], nc, ssem.at[sem(l, r, RS2)])
 
 
@@ -471,10 +470,8 @@
                 pltpu.VMEM((2 * nl - 1, 2) + tile, F32),
                 pltpu.VMEM((2,) + tile, BF16),
                 pltpu.VMEM((2, n) + tile, BF16),
-                pltpu.VMEM((nl, 2, nc * SUB, LANES), F32),
-                pltpu.VMEM((nl, 2, n) + tile, F32),
-                pltpu.VMEM((nl, 2, nc, LANES), F32),
-                pltpu.VMEM((nl, 2, n, LANES), F32),
+                pltpu.VMEM((nl, 2, nc * MSG, LANES), F32),
+                pltpu.VMEM((nl, 2, n * MSG, LANES), F32),
                 pltpu.VMEM((nl, 2, nc) + tile, F32),
                 pltpu.VMEM((nl, 2, nc) + tile, F32),
                 pltpu.VMEM((nl, 2, nc) + tile, F32),

time: 71.2 us -> 70.9 us (level)
  no operation moved by 1% of the time
where the time goes in v5:
time: 70.9 us; the launch traced here: 70.8 us
  Pallas kernels  70 us (99%)
  between operations  0.8 us (1%)
    pallas_call x1, Pallas kernels, local(): pl.pallas_call(functools.partial(_step_kernel, n, (nl, nb, s_dev, kvd, dh...  64 us
    pallas_call x1, Pallas kernels, local(): pl.pallas_call(_cache_kernel, out_shape=(jax.ShapeDtypeStruct((nb, D), BF...  5.95 us

profile of v5, /device:TPU:97, one launch (start us, length us, event | category | flops | bytes accessed | tf_op | source)
XLA Modules:
  0.0 70.8 jit_solution(15280064926813318207)
XLA Ops:
  0.6 64.0 %shard_map.139 = (bf16[16,2048]{1,0:T(8,128)(2,1)S(1)}, bf16[2,16,256,512]{3,2,1,0:T(8,128)(2,1)S(1)}, bf16[2,16,256,512]{3,2,1,0:T(8,128)(2,1)S(1)}) custom-call(s32[16]{0:T(128)} %lens.1, bf16[16,2048]{1,0:T(8,128)(2,1)} %x.1, bf16[2,2048]{1,0:T(2,128)(2,1)} %g1.1, bf16[2,2048]{1,0:T(2,128)(2,1)} %g2.1, bf16[2,2048,2048]{2,1,0:T(8,128)(2,1)} %wq.1, ...), custom_call_target="tpu_custom_call" | custom-call | tf_op jit(solution)/shard_map/pallas_call | solution.py:445
  64.7 6.0 %shard_map.140 = (bf16[16,2048]{1,0:T(8,128)(2,1)}, bf16[2,16,256,512]{3,2,1,0:T(8,128)(2,1)}, bf16[2,16,256,512]{3,2,1,0:T(8,128)(2,1)}) custom-call(bf16[16,2048]{1,0:T(8,128)(2,1)S(1)} %get-tuple-element.9.y_ref, bf16[2,16,256,512]{3,2,1,0:T(8,128)(2,1)S(1)} %get-tuple-element.10.k_ref, bf16[2,16,256,512]{3,2,1,0:T(8,128)(2,1)S(1)} %get-tuple-element.11.v_ref), custom_call_target="tpu_custom_call" | custom-call | tf_op jit(solution)/shard_map/pallas_call | solution.py:487
